TPU v7x, 128 devices: a whole 4x4x4 slice. The times are simulated.
128 devices in a mesh: dp: 2 (over core), fsdp: 64 (over z, y, x).
Axes of the slice: x: 4, y: 4, z: 4, core: 2. Of those that a mesh axis runs over, the one named last changes fastest.
Arguments:
- dec_in: bfloat16 [256, 512, 768], P(('dp', 'fsdp'))
- enc_out: bfloat16 [256, 768, 768], P(('dp', 'fsdp'))
- src_lens: int32 [256], P(('dp', 'fsdp'))
- tgt_lens: int32 [256], P(('dp', 'fsdp'))
- y_cot: bfloat16 [256, 512, 768], P(('dp', 'fsdp'))
- attn_w: bfloat16 [6144, 768], P('fsdp')
- ffn_w: bfloat16 [6144, 768], P('fsdp')
- vec_params: bfloat16 [14592], P('fsdp')
Outputs:
- output 1: bfloat16 [256, 512, 768], P(('dp', 'fsdp'))
- output 2: bfloat16 [256, 512, 768], P(('dp', 'fsdp'))
- output 3: bfloat16 [256, 768, 768], P(('dp', 'fsdp'))
- output 4: float32 [6144, 768], P('fsdp')
- output 5: float32 [6144, 768], P('fsdp')
- output 6: float32 [14592], P('fsdp')
All inputs are finite; a program needn't handle non-finite values.
Results may differ from a plain program's by a relative error of at most 0.016307.
Values are sent between devices in bfloat16 or wider.
A program may use at most 1 GiB of HBM per device.

v0:
```python
import jax
import jax.numpy as jnp
from jax import lax
from jax.sharding import PartitionSpec as P

HEAD_DIM = 64
LN_EPS = 1e-5
MASK_FILL = -1e30


def norm_fwd(resid_in, ln_gain, ln_shift):
    row_mean = jnp.mean(resid_in, axis=-1, keepdims=True)
    centred = resid_in - row_mean
    inv_std = lax.rsqrt(jnp.mean(centred * centred, axis=-1, keepdims=True) + LN_EPS)
    normed = centred * inv_std
    return (normed * ln_gain + ln_shift).astype(jnp.bfloat16), normed, inv_std


def norm_bwd(d_out, normed, inv_std, ln_gain):
    d_norm = d_out * ln_gain
    d_resid = inv_std * (d_norm - jnp.mean(d_norm, axis=-1, keepdims=True) - normed * jnp.mean(d_norm * normed, axis=-1, keepdims=True))
    return d_resid, jnp.sum(d_out * normed, axis=(0, 1)), jnp.sum(d_out, axis=(0, 1))


def attn_fwd(q_heads, k_heads, v_heads, key_mask):
    scores = jnp.einsum('bthe,bshe->bhts', q_heads, k_heads, preferred_element_type=jnp.float32)
    scores = jnp.where(key_mask[:, None], scores, MASK_FILL)
    attn_prob = jax.nn.softmax(scores, axis=-1)
    attn_out = jnp.einsum('bhts,bshe->bthe', attn_prob.astype(jnp.bfloat16), v_heads, preferred_element_type=jnp.float32)
    return attn_out.astype(jnp.bfloat16), attn_prob


def attn_bwd(d_out, q_heads, k_heads, v_heads, attn_prob):
    d_prob = jnp.einsum('bthe,bshe->bhts', d_out, v_heads, preferred_element_type=jnp.float32)
    d_value = jnp.einsum('bhts,bthe->bshe', attn_prob.astype(jnp.bfloat16), d_out, preferred_element_type=jnp.float32)
    d_score = (attn_prob * (d_prob - jnp.sum(attn_prob * d_prob, axis=-1, keepdims=True))).astype(jnp.bfloat16)
    d_query = jnp.einsum('bhts,bshe->bthe', d_score, k_heads, preferred_element_type=jnp.float32)
    d_key = jnp.einsum('bhts,bthe->bshe', d_score, q_heads, preferred_element_type=jnp.float32)
    return d_query, d_key, d_value


def gelu_grad(up_proj):
    norm_cdf = 0.5 * (1.0 + lax.erf(up_proj * 0.7071067811865476))
    norm_pdf = 0.3989422804014327 * jnp.exp(-0.5 * up_proj * up_proj)
    return norm_cdf + up_proj * norm_pdf


def unpack_params(attn_full, ffn_full, vec_full):
    d_model = attn_full.shape[1]
    ffn_dim = ffn_full.shape[0] // 2
    vec_f = vec_full.astype(jnp.float32)
    return dict(attn_mats=attn_full.reshape(8, d_model, d_model), w_up=ffn_full[:ffn_dim], w_down=ffn_full[ffn_dim:], biases=vec_f[:15 * d_model].reshape(15, d_model), up_bias=vec_f[15 * d_model:])


def layer_forward(dec_in, enc_out, src_lens, tgt_lens, weights):
    n_batch, n_tgt, d_model = dec_in.shape
    n_src = enc_out.shape[1]
    n_heads = d_model // HEAD_DIM
    attn_mats = weights['attn_mats']
    biases = weights['biases']
    tgt_pos = jnp.arange(n_tgt)
    self_mask = (tgt_pos[None, None, :] <= tgt_pos[None, :, None]) & (tgt_pos[None, None, :] < tgt_lens[:, None, None])
    cross_mask = jnp.arange(n_src)[None, None, :] < src_lens[:, None, None]
    q_scale = jnp.array([0.125, 1.0, 1.0], jnp.float32)[:, None]
    qkv_self = jnp.einsum('btd,nde->btne', dec_in, attn_mats[0:3], preferred_element_type=jnp.float32) + biases[0:3]
    qkv_self = (qkv_self * q_scale).astype(jnp.bfloat16).reshape(n_batch, n_tgt, 3, n_heads, HEAD_DIM)
    o_self, p_self = attn_fwd(qkv_self[:, :, 0], qkv_self[:, :, 1], qkv_self[:, :, 2], self_mask)
    o_self = o_self.reshape(n_batch, n_tgt, d_model)
    resid_one = dec_in.astype(jnp.float32) + jnp.einsum('btd,de->bte', o_self, attn_mats[3], preferred_element_type=jnp.float32) + biases[3]
    h_one, normed_one, inv_one = norm_fwd(resid_one, biases[9], biases[10])
    q_cross = ((jnp.einsum('btd,de->bte', h_one, attn_mats[4], preferred_element_type=jnp.float32) + biases[4]) * 0.125).astype(jnp.bfloat16).reshape(n_batch, n_tgt, n_heads, HEAD_DIM)
    kv_cross = (jnp.einsum('bsd,nde->bsne', enc_out, attn_mats[5:7], preferred_element_type=jnp.float32) + biases[5:7]).astype(jnp.bfloat16).reshape(n_batch, n_src, 2, n_heads, HEAD_DIM)
    o_cross, p_cross = attn_fwd(q_cross, kv_cross[:, :, 0], kv_cross[:, :, 1], cross_mask)
    o_cross = o_cross.reshape(n_batch, n_tgt, d_model)
    resid_two = h_one.astype(jnp.float32) + jnp.einsum('btd,de->bte', o_cross, attn_mats[7], preferred_element_type=jnp.float32) + biases[7]
    h_two, normed_two, inv_two = norm_fwd(resid_two, biases[11], biases[12])
    up_proj = jnp.einsum('btd,fd->btf', h_two, weights['w_up'], preferred_element_type=jnp.float32) + weights['up_bias']
    gelu_out = jax.nn.gelu(up_proj, approximate=False).astype(jnp.bfloat16)
    resid_three = h_two.astype(jnp.float32) + jnp.einsum('btf,fd->btd', gelu_out, weights['w_down'], preferred_element_type=jnp.float32) + biases[8]
    y_out, normed_three, inv_three = norm_fwd(resid_three, biases[13], biases[14])
    saved_acts = dict(qkv_self=qkv_self, p_self=p_self, o_self=o_self, normed_one=normed_one, inv_one=inv_one, h_one=h_one, q_cross=q_cross, kv_cross=kv_cross, p_cross=p_cross, o_cross=o_cross, normed_two=normed_two, inv_two=inv_two, h_two=h_two, up_proj=up_proj, gelu_out=gelu_out, normed_three=normed_three, inv_three=inv_three)
    return y_out, saved_acts


def layer_backward(y_cot, dec_in, enc_out, saved_acts, weights):
    n_batch, n_tgt, d_model = dec_in.shape
    n_src = enc_out.shape[1]
    n_heads = d_model // HEAD_DIM
    attn_mats = weights['attn_mats']
    biases = weights['biases']
    d_res3, g_gain3, g_shift3 = norm_bwd(y_cot.astype(jnp.float32), saved_acts['normed_three'], saved_acts['inv_three'], biases[13])
    d_res3_b = d_res3.astype(jnp.bfloat16)
    g_down = jnp.einsum('btf,btd->fd', saved_acts['gelu_out'], d_res3_b, preferred_element_type=jnp.float32)
    d_gelu = jnp.einsum('btd,fd->btf', d_res3_b, weights['w_down'], preferred_element_type=jnp.float32)
    d_up = d_gelu * gelu_grad(saved_acts['up_proj'])
    d_up_b = d_up.astype(jnp.bfloat16)
    g_up = jnp.einsum('btf,btd->fd', d_up_b, saved_acts['h_two'], preferred_element_type=jnp.float32)
    d_h2 = d_res3 + jnp.einsum('btf,fd->btd', d_up_b, weights['w_up'], preferred_element_type=jnp.float32)
    d_res2, g_gain2, g_shift2 = norm_bwd(d_h2, saved_acts['normed_two'], saved_acts['inv_two'], biases[11])
    d_res2_b = d_res2.astype(jnp.bfloat16)
    g_out_cross = jnp.einsum('btd,bte->de', saved_acts['o_cross'], d_res2_b, preferred_element_type=jnp.float32)
    d_o_cross = jnp.einsum('bte,de->btd', d_res2_b, attn_mats[7], preferred_element_type=jnp.float32).astype(jnp.bfloat16).reshape(n_batch, n_tgt, n_heads, HEAD_DIM)
    kv_cross = saved_acts['kv_cross']
    dq_cross, dk_cross, dv_cross = attn_bwd(d_o_cross, saved_acts['q_cross'], kv_cross[:, :, 0], kv_cross[:, :, 1], saved_acts['p_cross'])
    dq_cross = dq_cross.reshape(n_batch, n_tgt, d_model) * 0.125
    dq_cross_b = dq_cross.astype(jnp.bfloat16)
    g_q_cross = jnp.einsum('btd,bte->de', saved_acts['h_one'], dq_cross_b, preferred_element_type=jnp.float32)
    d_kv = jnp.stack([dk_cross, dv_cross], axis=2).reshape(n_batch, n_src, 2, d_model)
    d_kv_b = d_kv.astype(jnp.bfloat16)
    g_kv_cross = jnp.einsum('bsd,bsne->nde', enc_out, d_kv_b, preferred_element_type=jnp.float32)
    enc_grad = jnp.einsum('bsne,nde->bsd', d_kv_b, attn_mats[5:7], preferred_element_type=jnp.float32).astype(jnp.bfloat16)
    d_h1 = d_res2 + jnp.einsum('bte,de->btd', dq_cross_b, attn_mats[4], preferred_element_type=jnp.float32)
    d_res1, g_gain1, g_shift1 = norm_bwd(d_h1, saved_acts['normed_one'], saved_acts['inv_one'], biases[9])
    d_res1_b = d_res1.astype(jnp.bfloat16)
    g_out_self = jnp.einsum('btd,bte->de', saved_acts['o_self'], d_res1_b, preferred_element_type=jnp.float32)
    d_o_self = jnp.einsum('bte,de->btd', d_res1_b, attn_mats[3], preferred_element_type=jnp.float32).astype(jnp.bfloat16).reshape(n_batch, n_tgt, n_heads, HEAD_DIM)
    qkv_self = saved_acts['qkv_self']
    dq_self, dk_self, dv_self = attn_bwd(d_o_self, qkv_self[:, :, 0], qkv_self[:, :, 1], qkv_self[:, :, 2], saved_acts['p_self'])
    d_qkv = jnp.stack([dq_self * 0.125, dk_self, dv_self], axis=2).reshape(n_batch, n_tgt, 3, d_model)
    d_qkv_b = d_qkv.astype(jnp.bfloat16)
    g_qkv = jnp.einsum('btd,btne->nde', dec_in, d_qkv_b, preferred_element_type=jnp.float32)
    dec_grad = (d_res1 + jnp.einsum('btne,nde->btd', d_qkv_b, attn_mats[0:3], preferred_element_type=jnp.float32)).astype(jnp.bfloat16)
    g_attn = jnp.concatenate([g_qkv, g_out_self[None], g_q_cross[None], g_kv_cross, g_out_cross[None]], axis=0).reshape(8 * d_model, d_model)
    g_ffn = jnp.concatenate([g_up, g_down], axis=0)
    g_vec = jnp.concatenate([jnp.sum(d_qkv, axis=(0, 1)).reshape(-1), jnp.sum(d_res1, axis=(0, 1)), jnp.sum(dq_cross, axis=(0, 1)), jnp.sum(d_kv, axis=(0, 1)).reshape(-1), jnp.sum(d_res2, axis=(0, 1)), jnp.sum(d_res3, axis=(0, 1)), g_gain1, g_shift1, g_gain2, g_shift2, g_gain3, g_shift3, jnp.sum(d_up, axis=(0, 1))])
    return dec_grad, enc_grad, g_attn, g_ffn, g_vec


def solution(mesh):
    n_fsdp = mesh.shape['fsdp']
    n_dp = mesh.shape['dp']
    batch_axes = ('dp', 'fsdp')
    act_spec = P(batch_axes, None, None)
    len_spec = P(batch_axes)
    row_spec = P('fsdp', None)
    vec_spec = P('fsdp')

    def gather_all(attn_w, ffn_w, vec_params):
        return unpack_params(lax.all_gather(attn_w, 'fsdp', axis=0, tiled=True), lax.all_gather(ffn_w, 'fsdp', axis=0, tiled=True), lax.all_gather(vec_params, 'fsdp', axis=0, tiled=True))

    def device_step(dec_in, enc_out, src_lens, tgt_lens, y_cot, attn_w, ffn_w, vec_params):
        y_out, saved_acts = layer_forward(dec_in, enc_out, src_lens, tgt_lens, gather_all(attn_w, ffn_w, vec_params))
        attn_keep, ffn_keep, vec_keep, y_out = lax.optimization_barrier((attn_w, ffn_w, vec_params, y_out))
        dec_grad, enc_grad, g_attn, g_ffn, g_vec = layer_backward(y_cot, dec_in, enc_out, saved_acts, gather_all(attn_keep, ffn_keep, vec_keep))
        grad_scale = 1.0 / (dec_in.shape[0] * dec_in.shape[1] * n_fsdp * n_dp)
        grad_shards = [lax.psum(lax.psum_scatter(full_grad * grad_scale, 'fsdp', scatter_dimension=0, tiled=True), 'dp') for full_grad in (g_attn, g_ffn, g_vec)]
        return y_out, dec_grad, enc_grad, grad_shards[0], grad_shards[1], grad_shards[2]

    return jax.shard_map(device_step, mesh=mesh, in_specs=(act_spec, act_spec, len_spec, len_spec, act_spec, row_spec, row_spec, vec_spec), out_specs=(act_spec, act_spec, act_spec, row_spec, row_spec, vec_spec), check_vma=False)
```

profile of v0, /device:TPU:1, one launch (start us, length us, event | category | flops | bytes accessed | tf_op | source)
XLA Modules:
  0.0 1567.3 jit_solution(5410200954310397315)
XLA Ops:
  11.6 297.3 %all-reduce = bf16[14592]{0:T(1024)(128)(2,1)S(1)} all-reduce(bf16[14592]{0:T(1024)(128)(2,1)S(1)} %dynamic-update-slice), channel_id=1, replica_groups=mesh['dp'=2,'fsdp'=64] {'fsdp'}, use_global_device_ids=true, to_apply=%add | all-reduce | flops 14592 | bytes 58368
  320.0 6.7 copy.123
  326.6 14.8 fusion.101
  341.4 11.0 fusion.68
  371.4 18.4 %fusion.103 = (f32[2,12,512]{2,1,0:T(8,128)S(1)}, f32[2,12,512,768]{3,2,1,0:T(8,128)}) fusion(pred[2,768]{1,0:T(4,128)(4,1)S(1)} %iota_compare_fusion.1, bf16[2,512,12,64]{1,3,2,0:T(8,128)(2,1)} %bitcast.247, bf16[2,768,2,12,64]{1,4,3,2,0:T(8,128)(2,1)} %bitcast.265), kind=kOutput, calls=%fused_computation.198 | convolution fusion | flops 1236271872 | bytes 41731584 | tf_op jit(solution)/shard_map/sub | solution.py:28
  389.9 15.8 %fusion.71 = bf16[2,12,64,512]{3,2,1,0:T(8,128)(2,1)S(1)} fusion(bf16[2,768,2,12,64]{1,4,3,2,0:T(8,128)(2,1)} %bitcast.266, f32[2,12,512,768]{3,2,1,0:T(8,128)} %get-tuple-element.57, f32[2,12,512]{2,1,0:T(8,128)S(1)} %get-tuple-element.56), kind=kOutput, calls=%fused_computation.133 | convolution fusion | flops 1227620352 | bytes 41730048 | tf_op jit(solution)/shard_map/bhts,bshe->bthe/dot_general | solution.py:29
  410.8 14.6 fusion.56
  425.4 31.0 %fusion.14 = bf16[2,512,3072]{2,1,0:T(8,128)(2,1)S(1)} fusion(f32[2,512,3072]{2,1,0:T(8,128)} %get-tuple-element.60, f32[3072]{0:T(1024)S(1)} %copy-done.29, u8[512,3072]{1,0:T(8,128)(4,1)S(1)} %get-tuple-element.15, u8[512,3072]{1,0:T(8,128)(4,1)S(1)} %get-tuple-element.14), kind=kLoop, calls=%fused_computation.21 | loop fusion | flops 223346688 | bytes 22032384 | tf_op jit(solution)/shard_map/convert_element_type | solution.py:78
  466.2 287.9 %all-reduce.1 = bf16[14592]{0:T(1024)(128)(2,1)S(1)} all-reduce(bf16[14592]{0:T(1024)(128)(2,1)S(1)} %dynamic-update-slice.1), channel_id=1, replica_groups=mesh['dp'=2,'fsdp'=64] {'fsdp'}, use_global_device_ids=true, to_apply=%add.1 | all-reduce | flops 14592 | bytes 58368
  758.4 12.2 convolution_bitcast_fusion
  770.6 13.2 fusion.106
  789.8 10.2 maximum_multiply_fusion
  800.2 12.1 multiply_reduce_fusion.2
  822.5 16.4 %fusion.28 = f32[2,12,64,768]{3,2,1,0:T(8,128)} fusion(bf16[2,512,12,64]{1,3,2,0:T(8,128)(2,1)} %bitcast.259, f32[2,12,512,768]{3,2,1,0:T(8,128)} %get-tuple-element.57, f32[2,12,512]{2,1,0:T(8,128)S(1)} %get-tuple-element.56), kind=kOutput, calls=%fused_computation.51 | convolution fusion | flops 1226833920 | bytes 44089344 | tf_op jit(solution)/shard_map/bhts,bthe->bshe/dot_general | solution.py:35
  845.0 25.2 %multiply_reduce_fusion = (f32[2,12,512]{2,1,0:T(8,128)S(1)}, f32[2,12,512,768]{3,2,1,0:T(8,128)}) fusion(f32[2,12,512,768]{3,2,1,0:T(8,128)} %get-tuple-element.57, f32[2,12,512]{2,1,0:T(8,128)S(1)} %get-tuple-element.56, bf16[2,512,12,64]{1,3,2,0:T(8,128)(2,1)} %bitcast.260, bf16[2,768,2,12,64]{1,4,3,2,0:T(8,128)(2,1)} %bitcast.267), kind=kOutput, calls=%fused_computation.3 | convolution fusion | flops 1236258816 | bytes 79527936 | tf_op jit(solution)/shard_map/bthe,bshe->bhts/dot_general | solution.py:34
  870.2 30.8 %multiply_convert_fusion = bf16[2,12,512,768]{3,2,1,0:T(8,128)(2,1)} fusion(f32[2,12,512,768]{3,2,1,0:T(8,128)} %get-tuple-element.65, f32[2,12,512]{2,1,0:T(8,128)S(1)} %get-tuple-element.64, f32[2,12,512,768]{3,2,1,0:T(8,128)} %get-tuple-element.57, f32[2,12,512]{2,1,0:T(8,128)S(1)} %get-tuple-element.56), kind=kLoop, calls=%fused_computation.2 | loop fusion | flops 37748736 | bytes 94470144 | tf_op jit(solution)/shard_map/convert_element_type | solution.py:36
  901.0 11.9 fusion.107
  912.8 6.2 copy.97
  919.1 11.8 multiply_convert_fusion.4
  945.3 14.2 fusion.36
  963.1 17.7 %multiply_reduce_fusion.1 = (f32[2,12,512]{2,1,0:T(8,128)S(1)}, f32[2,12,512,512]{2,3,1,0:T(8,128)}) fusion(f32[2,12,512,512]{2,3,1,0:T(8,128)} %get-tuple-element.53, f32[2,12,512]{2,1,0:T(8,128)S(1)} %copy-done.28, bf16[2,512,12,64]{1,3,2,0:T(8,128)(2,1)} %bitcast.262, bf16[2,512,3,12,64]{1,4,3,0,2:T(8,128)(2,1)} %bitcast.243), kind=kOutput, calls=%fused_computation.8 | convolution fusion | flops 824168448 | bytes 53575680 | tf_op jit(solution)/shard_map/bthe,bshe->bhts/dot_general | solution.py:34
  980.9 17.1 %multiply_convert_fusion.1 = bf16[2,12,512,512]{2,3,1,0:T(8,128)(2,1)S(1)} fusion(f32[2,12,512,512]{2,3,1,0:T(8,128)} %get-tuple-element.69, f32[2,12,512]{2,1,0:T(8,128)S(1)} %get-tuple-element.68, f32[2,12,512,512]{2,3,1,0:T(8,128)} %get-tuple-element.53, f32[2,12,512]{2,1,0:T(8,128)S(1)} %copy-done.28), kind=kLoop, calls=%fused_computation.7 | loop fusion | flops 25165824 | bytes 63012864 | tf_op jit(solution)/shard_map/convert_element_type | solution.py:36
  997.9 6.3 convolution_multiply_fusion
  1007.8 10.6 fusion.77
  1022.0 7.8 bitcast_dynamic-update-slice_fusion
  1034.4 6.4 bitcast_dynamic-update-slice_fusion.1
  1043.6 6.8 broadcast_multiply_fusion
  1065.3 287.1 %all-reduce.2 = f32[14592]{0:T(1024)S(1)} all-reduce(f32[14592]{0:T(1024)S(1)} %broadcast_multiply_fusion.1), channel_id=4, replica_groups=mesh['dp'=2,'fsdp'=64] {'fsdp'}, use_global_device_ids=true, to_apply=%region_35.36.clone | all-reduce | flops 14592 | bytes 116736
  1359.7 168.5 %psum.23 = f32[228]{0:T(256)} all-reduce(f32[228]{0:T(256)S(1)} %dynamic-slice.3), channel_id=1, replica_groups=mesh['dp'=2,'fsdp'=64] {'dp'}, use_global_device_ids=true, to_apply=%region_36.37 | all-reduce | flops 228 | bytes 1824 | tf_op jit(solution)/shard_map/psum | solution.py:146
  1528.2 10.7 fusion.52
  1538.9 9.8 bitcast_convert_fusion
  1548.6 8.0 all-reduce.6.cloned.1.call-done
  (234 shorter events, 131.9 us)
Async XLA Ops:
  7.2 357.0 %copy-start = (bf16[2,768,768]{2,1,0:T(8,128)(2,1)S(1)}, bf16[2,768,768]{2,1,0:T(8,128)(2,1)}, u32[]{:S(2)}) copy-start(bf16[2,768,768]{2,1,0:T(8,128)(2,1)} %param.10) | copy-start | bytes 7077892
  7.2 304.8 %all-gather.5.cloned.1.call-start = ((), (), s32[]{:S(2)}) async-start(), calls=%async_computation.2 | async-start | bytes 9584640 | tf_op jit(solution)/shard_map/all_gather | solution.py:139
  7.9 402.8 %all-gather.7.cloned.1.call-start = ((), (), s32[]{:S(2)}) async-start(), calls=%async_computation.3 | async-start | bytes 9584640 | tf_op jit(solution)/shard_map/all_gather | solution.py:139
  8.7 762.0 %all-gather.9.cloned.1.call-start = ((), (), s32[]{:S(2)}) async-start(), calls=%async_computation.4 | async-start | bytes 9584640 | tf_op jit(solution)/shard_map/all_gather | solution.py:139
  341.4 11.1 copy-start.27
  341.4 11.1 copy-start.48
  371.4 34.3 %slice-start.5 = ((s8[9437184]{0:T(1024)(128)(4,1)}), s8[1048576]{0:T(1024)(128)(4,1)S(1)}, s32[]{:S(2)}) async-start(s8[9437184]{0:T(1024)(128)(4,1)} %bitcast.252), calls=%async_computation.14 | async-start | bytes 2097152
  389.9 15.9 %slice-start.6 = ((s8[9437184]{0:T(1024)(128)(4,1)}), s8[4194304]{0:T(1024)(128)(4,1)S(1)}, s32[]{:S(2)}) async-start(s8[9437184]{0:T(1024)(128)(4,1)} %bitcast.252), calls=%async_computation.15 | async-start | bytes 8388608
  389.9 15.9 %slice-start.7 = ((s8[9437184]{0:T(1024)(128)(4,1)}), s8[4194304]{0:T(1024)(128)(4,1)S(1)}, s32[]{:S(2)}) async-start(s8[9437184]{0:T(1024)(128)(4,1)} %bitcast.252), calls=%async_computation.16 | async-start | bytes 8388608
  389.9 15.9 %copy-start.16 = (bf16[2,512,768]{2,1,0:T(8,128)(2,1)S(1)}, bf16[2,512,768]{2,1,0:T(8,128)(2,1)}, u32[]{:S(2)}) copy-start(bf16[2,512,768]{2,1,0:T(8,128)(2,1)} %copy-done.15) | copy-start | bytes 4718596
  425.4 31.1 %copy-start.18 = (bf16[2,512,768]{2,1,0:T(8,128)(2,1)S(1)}, bf16[2,512,768]{2,1,0:T(8,128)(2,1)}, u32[]{:S(2)}) copy-start(bf16[2,512,768]{2,1,0:T(8,128)(2,1)} %add_convert_fusion.2) | copy-start | bytes 4718596
  425.4 31.1 %copy-start.43 = (f32[768]{0:T(1024)S(1)}, f32[768]{0:T(1024)}, u32[]{:S(2)}) copy-start(f32[768]{0:T(1024)} %get-tuple-element.42) | copy-start | bytes 9220
  425.4 31.1 %copy-start.46 = (bf16[6144,768]{1,0:T(8,128)(2,1)S(1)}, bf16[6144,768]{1,0:T(8,128)(2,1)}, u32[]{:S(2)}) copy-start(bf16[6144,768]{1,0:T(8,128)(2,1)} %all-gather.7.cloned.1.call-done) | copy-start | bytes 28311556
  461.8 338.3 %copy-start.21 = (f32[2,512]{1,0:T(2,128)}, f32[2,512]{1,0:T(2,128)S(1)}, u32[]{:S(2)}) copy-start(f32[2,512]{1,0:T(2,128)S(1)} %broadcast_multiply_fusion.8) | copy-start | bytes 12292
  462.4 337.7 %copy-start.25 = (f32[2,512]{1,0:T(2,128)}, f32[2,512]{1,0:T(2,128)S(1)}, u32[]{:S(2)}) copy-start(f32[2,512]{1,0:T(2,128)S(1)} %add_rsqrt_fusion) | copy-start | bytes 12292
  465.3 349.8 %all-gather.11.cloned.1.call-start = ((), (), s32[]{:S(2)}) async-start(), calls=%async_computation.5 | async-start | bytes 9584640 | tf_op jit(solution)/shard_map/all_gather | solution.py:139
  465.9 1073.0 %reduce-scatter.5.cloned.1.call-start = ((), (), s32[]{:S(2)}) async-start(), calls=%async_computation.7 | async-start | bytes 19169280 | tf_op jit(solution)/shard_map/reduce_scatter | solution.py:146
  754.7 45.4 %copy-start.32 = (f32[768]{0:T(1024)}, f32[768]{0:T(1024)S(1)}, u32[]{:S(2)}) copy-start(f32[768]{0:T(1024)S(1)} %get-tuple-element.39) | copy-start | bytes 9220
  758.4 41.7 %copy-start.37 = (f32[2,512]{1,0:T(2,128)}, f32[2,512]{1,0:T(2,128)S(1)}, u32[]{:S(2)}) copy-start(f32[2,512]{1,0:T(2,128)S(1)} %get-tuple-element.72) | copy-start | bytes 12292
  758.4 41.7 %copy-start.39 = (f32[2,512]{1,0:T(2,128)}, f32[2,512]{1,0:T(2,128)S(1)}, u32[]{:S(2)}) copy-start(f32[2,512]{1,0:T(2,128)S(1)} %get-tuple-element.73) | copy-start | bytes 12292
  770.6 13.2 copy-start.19
  800.1 738.8 %reduce-scatter.3.cloned.1.call-start = ((), (), s32[]{:S(2)}) async-start(), calls=%async_computation.6 | async-start | bytes 19169280 | tf_op jit(solution)/shard_map/reduce_scatter | solution.py:146
  800.2 12.1 copy-start.7
  870.2 30.8 %copy-start.9 = (bf16[2,512,768]{1,2,0:T(8,128)(2,1)S(1)}, bf16[2,512,768]{1,2,0:T(8,128)(2,1)}, u32[]{:S(2)}) copy-start(bf16[2,512,768]{1,2,0:T(8,128)(2,1)} %copy.85) | copy-start | bytes 4718596
  919.1 11.8 copy-start.24
  919.1 11.8 copy-start.31
  919.1 11.8 copy-start.41
  1018.4 15.9 %slice-start = ((s8[4718592]{0:T(1024)(128)(4,1)}), s8[524288]{0:T(1024)(128)(4,1)S(1)}, s32[]{:S(2)}) async-start(s8[4718592]{0:T(1024)(128)(4,1)} %bitcast.239), calls=%async_computation.9 | async-start | bytes 1048576
  1022.0 7.8 copy-start.13
  1022.0 12.3 slice-start.1
  1034.4 6.4 copy-start.14
  1050.5 506.2 %all-reduce.6.cloned.1.call-start = ((), (), s32[]{:S(2)}) async-start(), calls=%async_computation.8 | async-start | bytes 1179648 | tf_op jit(solution)/shard_map/psum | solution.py:146
  (39 other events, 115.2 us)
Sparse Core Ops, SparseCore 0:
  10.7 84.5 all-gather.4
  98.1 81.2 all-gather.6
  465.4 129.6 all-gather.8
  597.7 81.1 all-gather.10
  800.2 341.1 reduce-scatter.4
  1145.9 246.1 reduce-scatter.2
  1539.0 17.6 all-reduce.5
where the time goes:
time: 1580 us; the launch traced here: 1570 us
  blocking collectives  1040 us (66%)
  matrix products  311 us (20%)
  other arithmetic  124 us (8%)
  local copies, waits for them, and re-layouts  63.5 us (4%)
  between operations  16.8 us (1%)
    unnamed x3, blocking collectives  872 us
    psum x1, blocking collectives, device_step(): lax.psum(lax.psum_scatter(full_grad * grad_scale, 'fsdp', scatter_dimensi...  168 us
    convert_element_type x2, other arithmetic, attn_bwd(): (attn_prob * (d_prob - jnp.sum(attn_prob * d_prob, axis=-1, keepdims=True...  47.8 us
    dot_general x2, matrix products, attn_bwd(): jnp.einsum('bthe,bshe->bhts', d_out, v_heads, preferred_element_type=jnp....  42.9 us
    sub x2, matrix products, attn_fwd(): attn_prob = jax.nn.softmax(scores, axis=-1)  33.2 us
  transfers between devices with their start and end apart: 7, of which 1 were waited for; matrix products, arithmetic and copies ran while one was open for 28% of the time, Pallas kernels for 0%

commit v1 on v0

--- a/solution.py
+++ b/solution.py
@@ -130,20 +130,35 @@
     n_fsdp = mesh.shape['fsdp']
     n_dp = mesh.shape['dp']
     batch_axes = ('dp', 'fsdp')
+    all_axes = ('fsdp', 'dp')
     act_spec = P(batch_axes, None, None)
     len_spec = P(batch_axes)
     row_spec = P('fsdp', None)
     vec_spec = P('fsdp')
 
-    def gather_all(attn_w, ffn_w, vec_params):
-        return unpack_params(lax.all_gather(attn_w, 'fsdp', axis=0, tiled=True), lax.all_gather(ffn_w, 'fsdp', axis=0, tiled=True), lax.all_gather(vec_params, 'fsdp', axis=0, tiled=True))
+    def gather_rows(w_rows):
+        half = w_rows.shape[0] // n_dp
+        mine = lax.dynamic_slice_in_dim(w_rows, lax.axis_index('dp') * half, half, 0)
+        return lax.all_gather(mine, all_axes, axis=0, tiled=True)
+
+    def gather_vec(vec_rows):
+        n_own = vec_rows.shape[0]
+        mine = jnp.where(lax.axis_index('dp') == 0, vec_rows, jnp.zeros_like(vec_rows))
+        full = lax.dynamic_update_slice_in_dim(jnp.zeros((n_own * n_fsdp,), vec_rows.dtype), mine, lax.axis_index('fsdp') * n_own, 0)
+        return lax.psum(full, all_axes)
+
+    def scatter_rows(full_grad):
+        return lax.all_gather(lax.psum_scatter(full_grad, all_axes, scatter_dimension=0, tiled=True), 'dp', axis=0, tiled=True)
+
+    def scatter_vec(full_grad):
+        n_own = full_grad.shape[0] // n_fsdp
+        return lax.dynamic_slice_in_dim(lax.psum(full_grad, all_axes), lax.axis_index('fsdp') * n_own, n_own, 0)
 
     def device_step(dec_in, enc_out, src_lens, tgt_lens, y_cot, attn_w, ffn_w, vec_params):
-        y_out, saved_acts = layer_forward(dec_in, enc_out, src_lens, tgt_lens, gather_all(attn_w, ffn_w, vec_params))
-        attn_keep, ffn_keep, vec_keep, y_out = lax.optimization_barrier((attn_w, ffn_w, vec_params, y_out))
-        dec_grad, enc_grad, g_attn, g_ffn, g_vec = layer_backward(y_cot, dec_in, enc_out, saved_acts, gather_all(attn_keep, ffn_keep, vec_keep))
+        weights = unpack_params(gather_rows(attn_w), gather_rows(ffn_w), gather_vec(vec_params))
+        y_out, saved_acts = layer_forward(dec_in, enc_out, src_lens, tgt_lens, weights)
+        dec_grad, enc_grad, g_attn, g_ffn, g_vec = layer_backward(y_cot, dec_in, enc_out, saved_acts, weights)
         grad_scale = 1.0 / (dec_in.shape[0] * dec_in.shape[1] * n_fsdp * n_dp)
-        grad_shards = [lax.psum(lax.psum_scatter(full_grad * grad_scale, 'fsdp', scatter_dimension=0, tiled=True), 'dp') for full_grad in (g_attn, g_ffn, g_vec)]
-        return y_out, dec_grad, enc_grad, grad_shards[0], grad_shards[1], grad_shards[2]
+        return y_out, dec_grad, enc_grad, scatter_rows(g_attn * grad_scale), scatter_rows(g_ffn * grad_scale), scatter_vec(g_vec * grad_scale)
 
     return jax.shard_map(device_step, mesh=mesh, in_specs=(act_spec, act_spec, len_spec, len_spec, act_spec, row_spec, row_spec, vec_spec), out_specs=(act_spec, act_spec, act_spec, row_spec, row_spec, vec_spec), check_vma=False)

time: 1580 us -> 845 us (0.53)
  blocking collectives: 1040 us -> 142 us
  waiting for transfers between devices: 10 us -> 197 us
    unnamed x3 -> x0, blocking collectives: 872 us -> none
    reduce_scatter x2, waiting for transfers between devices: 0.01 us -> 195 us  [scatter_rows(): lax.psum_scatter(full_grad, all_axes, scatter_dimension=0, tiled=True)]
    psum x1 -> x2, blocking collectives: 168 us -> 135 us  [the longest x1 70.1 us: gather_vec(): return lax.psum(full, all_axes)]
  transfers between devices with their start and end apart: 7 -> 4, of which waited for: 1 -> 2; matrix products, arithmetic and copies ran while one was open for 28% -> 36% of each run, Pallas kernels for 0% -> 0%
where the time goes in v1:
time: 845 us; the launch traced here: 837 us
  matrix products  312 us (37%)
  waiting for transfers between devices  197 us (23%)
  blocking collectives  142 us (17%)
  other arithmetic  122 us (14%)
  local copies, waits for them, and re-layouts  49.8 us (6%)
  between operations  15 us (2%)
    reduce_scatter x2, waiting for transfers between devices, scatter_rows(): lax.psum_scatter(full_grad, all_axes, scatter_dimension=0, tiled=True)  195 us
    psum x1, blocking collectives, gather_vec(): return lax.psum(full, all_axes)  70.1 us
    psum x1, blocking collectives, scatter_vec(): lax.psum(full_grad, all_axes)  65.3 us
    convert_element_type x2, other arithmetic, attn_bwd(): (attn_prob * (d_prob - jnp.sum(attn_prob * d_prob, axis=-1, keepdims=True...  47.6 us
    dot_general x2, matrix products, attn_bwd(): jnp.einsum('bthe,bshe->bhts', d_out, v_heads, preferred_element_type=jnp....  43.3 us
    sub x2, matrix products, attn_fwd(): attn_prob = jax.nn.softmax(scores, axis=-1)  33.8 us
    convert_element_type x1, other arithmetic, layer_forward(): gelu_out = jax.nn.gelu(up_proj, approximate=False).astype(jnp.bfloat16)  31 us
    dot_general x2, matrix products, attn_bwd(): jnp.einsum('bhts,bthe->bshe', attn_prob.astype(jnp.bfloat16), d_out, pref...  30.6 us
  transfers between devices with their start and end apart: 4, of which 2 were waited for; matrix products, arithmetic and copies ran while one was open for 36% of the time, Pallas kernels for 0%

profile of v1, /device:TPU:1, one launch (start us, length us, event | category | flops | bytes accessed | tf_op | source)
XLA Modules:
  0.0 837.4 jit_solution(9640093586830568471)
XLA Ops:
  10.9 70.1 %psum.14 = bf16[14592]{0:T(1024)(128)(2,1)S(1)} all-reduce(bf16[14592]{0:T(1024)(128)(2,1)S(1)} %dynamic_update_slice.3), channel_id=1, replica_groups=mesh['dp'=2,'fsdp'=64] {'fsdp','dp'}, use_global_device_ids=true, to_apply=%region_0.1 | all-reduce | flops 14592 | bytes 58368 | tf_op jit(solution)/shard_map/psum | solution.py:148
  88.2 6.9 multiply_convert_fusion.2
  95.1 15.3 %fusion.99 = (f32[2,12,512]{2,1,0:T(8,128)S(1)}, f32[2,12,512,512]{2,3,1,0:T(8,128)}) fusion(pred[2,512,512]{1,2,0:T(8,128)(4,1)S(1)} %broadcast_and_fusion, bf16[2,512,3,12,64]{1,4,3,0,2:T(8,128)(2,1)} %bitcast.232), kind=kOutput, calls=%fused_computation.191 | convolution fusion | flops 824181248 | bytes 28884992 | tf_op jit(solution)/shard_map/sub | solution.py:28
  110.4 11.1 %fusion.68 = bf16[2,12,64,512]{3,2,1,0:T(8,128)(2,1)S(1)} fusion(bf16[2,512,3,12,64]{1,4,3,0,2:T(8,128)(2,1)} %bitcast.233, f32[2,12,512,512]{2,3,1,0:T(8,128)} %get-tuple-element.39, f32[2,12,512]{2,1,0:T(8,128)S(1)} %get-tuple-element.38), kind=kOutput, calls=%fused_computation.129 | convolution fusion | flops 818675712 | bytes 28360704 | tf_op jit(solution)/shard_map/bhts,bshe->bthe/dot_general | solution.py:29
  136.1 6.2 add_convert_fusion
  142.3 18.5 %fusion.101 = (f32[2,12,512]{2,1,0:T(8,128)S(1)}, f32[2,12,512,768]{3,2,1,0:T(8,128)}) fusion(pred[2,768]{1,0:T(4,128)(4,1)S(1)} %iota_compare_fusion.1, bf16[2,512,12,64]{1,3,2,0:T(8,128)(2,1)} %bitcast.221, bf16[2,768,2,12,64]{1,4,3,0,2:T(8,128)(2,1)} %bitcast.226), kind=kOutput, calls=%fused_computation.193 | convolution fusion | flops 1236271872 | bytes 41731584 | tf_op jit(solution)/shard_map/sub | solution.py:28
  160.8 14.9 %fusion.71 = bf16[2,12,64,512]{3,2,1,0:T(8,128)(2,1)S(1)} fusion(bf16[2,768,2,12,64]{1,4,3,0,2:T(8,128)(2,1)} %bitcast.227, f32[2,12,512,768]{3,2,1,0:T(8,128)} %get-tuple-element.43, f32[2,12,512]{2,1,0:T(8,128)S(1)} %get-tuple-element.42), kind=kOutput, calls=%fused_computation.130 | convolution fusion | flops 1227620352 | bytes 41730048 | tf_op jit(solution)/shard_map/bhts,bshe->bthe/dot_general | solution.py:29
  182.5 14.4 %fusion.56 = (u8[512,3072]{1,0:T(8,128)(4,1)S(1)}, u8[512,3072]{1,0:T(8,128)(4,1)S(1)}, f32[2,512,3072]{2,1,0:T(8,128)}) fusion(f32[3072]{0:T(1024)S(1)} %slice.189, bf16[2,512,768]{2,1,0:T(8,128)(2,1)} %add_convert_fusion.2, bf16[6144,768]{1,0:T(8,128)(2,1)} %all-gather.5.cloned.1.call-done), kind=kOutput, calls=%fused_computation.107 | convolution fusion | flops 4872732672 | bytes 22032384 | tf_op jit(solution)/shard_map/btd,fd->btf/dot_general | solution.py:77
  197.0 31.0 %fusion.14 = bf16[2,512,3072]{2,1,0:T(8,128)(2,1)S(1)} fusion(f32[2,512,3072]{2,1,0:T(8,128)} %get-tuple-element.46, f32[3072]{0:T(1024)S(1)} %slice.189, u8[512,3072]{1,0:T(8,128)(4,1)S(1)} %get-tuple-element.7, u8[512,3072]{1,0:T(8,128)(4,1)S(1)} %get-tuple-element.6), kind=kLoop, calls=%fused_computation.21 | loop fusion | flops 223346688 | bytes 22032384 | tf_op jit(solution)/shard_map/convert_element_type | solution.py:78
  228.0 7.6 fusion.103
  239.3 8.9 %convolution_bitcast_fusion = f32[3072,768]{1,0:T(8,128)} fusion(bf16[2,512,3072]{2,1,0:T(8,128)(2,1)S(1)} %fusion.14, bf16[2,512,768]{2,1,0:T(8,128)(2,1)S(1)} %copy-done.11, f32[2,512,768]{2,1,0:T(8,128)S(1)} %get-tuple-element.48, f32[2,512]{1,0:T(2,128)S(1)} %get-tuple-element.57, f32[2,512]{1,0:T(2,128)S(1)} %get-tuple-element.58, ...), kind=kOutput, calls=%fused_computation.66 | convolution fusion | flops 4838916096 | bytes 20466688 | tf_op jit(solution)/shard_map/btf,btd->fd/dot_general | solution.py:93
  248.3 14.1 %fusion.104 = (f32[3072]{0:T(1024)}, bf16[2,512,3072]{2,1,0:T(8,128)(2,1)}) fusion(f32[2,512,3072]{2,1,0:T(8,128)S(1)} %bitcast.219, f32[3072]{0:T(1024)S(1)} %slice.189, bf16[6144,768]{1,0:T(8,128)(2,1)} %all-gather.5.cloned.1.call-done, f32[2,512]{1,0:T(2,128)S(1)} %get-tuple-element.57, f32[2,512,768]{2,1,0:T(8,128)S(1)} %get-tuple-element.48, ...), kind=kOutput, calls=%fused_computation.196 | convolution fusion | flops 4876661760 | bytes 28355584 | tf_op jit(solution)/shard_map/btd,fd->btf/dot_general | solution.py:94
  262.3 10.4 %convolution_bitcast_fusion.1 = f32[3072,768]{1,0:T(8,128)} fusion(bf16[2,512,768]{2,1,0:T(8,128)(2,1)S(1)} %copy-done.24, bf16[2,512,3072]{2,1,0:T(8,128)(2,1)} %get-tuple-element.56), kind=kOutput, calls=%fused_computation.67 | convolution fusion | flops 4831838208 | bytes 17301504 | tf_op jit(solution)/shard_map/btf,btd->fd/dot_general | solution.py:97
  272.8 8.9 %multiply_reduce_fusion.2 = (f32[768]{0:T(1024)}, f32[2,512]{1,0:T(2,128)S(1)}, f32[2,512]{1,0:T(2,128)S(1)}, f32[768]{0:T(1024)}, f32[2,512,768]{2,1,0:T(8,128)S(1)}) fusion(f32[2,512,768]{2,1,0:T(8,128)S(1)} %copy-done.5, f32[2,512]{1,0:T(2,128)S(1)} %add_rsqrt_fusion.1, f32[2,512]{1,0:T(2,128)S(1)} %broadcast_multiply_fusion.9, ...), kind=kOutput, calls=%fused_computation.88 | convolution fusion | flops 4845989888 | bytes 22065152 | tf_op jit(solution)/shard_map/btf,fd->btd/dot_general | solution.py:98
  291.5 16.4 %fusion.28 = f32[2,12,64,768]{3,2,1,0:T(8,128)} fusion(bf16[2,512,12,64]{1,3,2,0:T(8,128)(2,1)} %bitcast.242, f32[2,12,512,768]{3,2,1,0:T(8,128)} %get-tuple-element.43, f32[2,12,512]{2,1,0:T(8,128)S(1)} %get-tuple-element.42), kind=kOutput, calls=%fused_computation.51 | convolution fusion | flops 1226833920 | bytes 44089344 | tf_op jit(solution)/shard_map/bhts,bthe->bshe/dot_general | solution.py:35
  307.9 25.2 %multiply_reduce_fusion = (f32[2,12,512]{2,1,0:T(8,128)S(1)}, f32[2,12,512,768]{3,2,1,0:T(8,128)}) fusion(f32[2,12,512,768]{3,2,1,0:T(8,128)} %get-tuple-element.43, f32[2,12,512]{2,1,0:T(8,128)S(1)} %get-tuple-element.42, bf16[2,512,12,64]{1,3,2,0:T(8,128)(2,1)} %bitcast.243, bf16[2,768,2,12,64]{1,4,3,0,2:T(8,128)(2,1)} %bitcast.228), kind=kOutput, calls=%fused_computation.3 | convolution fusion | flops 1236258816 | bytes 79527936 | tf_op jit(solution)/shard_map/bthe,bshe->bhts/dot_general | solution.py:34
  333.1 6.1 copy.59
  339.2 14.0 %maximum_multiply_fusion = f32[6144,768]{1,0:T(8,128)} fusion(f32[3072,768]{1,0:T(8,128)} %convolution_bitcast_fusion, f32[3072,768]{1,0:T(8,128)} %convolution_bitcast_fusion.1), kind=kLoop, calls=%fused_computation.14 | loop fusion | flops 9437184 | bytes 37748736 | tf_op jit(solution)/shard_map/mul | solution.py:162
  353.3 30.8 %multiply_convert_fusion = bf16[2,12,512,768]{3,2,1,0:T(8,128)(2,1)} fusion(f32[2,12,512,768]{3,2,1,0:T(8,128)} %get-tuple-element.51, f32[2,12,512]{2,1,0:T(8,128)S(1)} %get-tuple-element.50, f32[2,12,512,768]{3,2,1,0:T(8,128)} %get-tuple-element.43, f32[2,12,512]{2,1,0:T(8,128)S(1)} %get-tuple-element.42), kind=kLoop, calls=%fused_computation.2 | loop fusion | flops 37748736 | bytes 94470144 | tf_op jit(solution)/shard_map/convert_element_type | solution.py:36
  384.1 11.9 %fusion.105 = f32[2,12,64,768]{3,2,1,0:T(8,128)} fusion(bf16[2,512,12,64]{1,3,2,0:T(8,128)(2,1)S(1)} %bitcast.222, bf16[2,12,512,768]{3,2,1,0:T(8,128)(2,1)} %multiply_convert_fusion), kind=kOutput, calls=%fused_computation.197 | convolution fusion | flops 1207959552 | bytes 25165824 | tf_op jit(solution)/shard_map/bhts,bthe->bshe/dot_general | solution.py:38
  402.0 10.6 %multiply_reduce_fusion.9 = (f32[12,64]{1,0:T(8,128)S(1)}, bf16[2,12,64,512]{3,2,1,0:T(8,128)(2,1)S(1)}) fusion(bf16[2,12,512,768]{3,2,1,0:T(8,128)(2,1)} %multiply_convert_fusion, bf16[2,768,2,12,64]{1,4,3,0,2:T(8,128)(2,1)} %bitcast.229), kind=kOutput, calls=%fused_computation.108 | convolution fusion | flops 1210318080 | bytes 22809600 | tf_op jit(solution)/shard_map/bhts,bshe->bthe/dot_general | solution.py:37
  427.2 14.2 %fusion.36 = f32[2,12,64,512]{3,2,1,0:T(8,128)} fusion(bf16[2,512,12,64]{1,3,2,0:T(8,128)(2,1)} %bitcast.240, f32[2,12,512,512]{2,3,1,0:T(8,128)} %get-tuple-element.39, f32[2,12,512]{2,1,0:T(8,128)S(1)} %copy-done.30), kind=kOutput, calls=%fused_computation.62 | convolution fusion | flops 817889280 | bytes 29933568 | tf_op jit(solution)/shard_map/bhts,bthe->bshe/dot_general | solution.py:35
  445.0 18.1 %multiply_reduce_fusion.1 = (f32[2,12,512]{2,1,0:T(8,128)S(1)}, f32[2,12,512,512]{2,3,1,0:T(8,128)}) fusion(f32[2,12,512,512]{2,3,1,0:T(8,128)} %get-tuple-element.39, f32[2,12,512]{2,1,0:T(8,128)S(1)} %copy-done.30, bf16[2,512,12,64]{1,3,2,0:T(8,128)(2,1)} %bitcast.241, bf16[2,512,3,12,64]{1,4,3,0,2:T(8,128)(2,1)} %bitcast.234), kind=kOutput, calls=%fused_computation.8 | convolution fusion | flops 824168448 | bytes 53575680 | tf_op jit(solution)/shard_map/bthe,bshe->bhts/dot_general | solution.py:34
  463.1 16.8 %multiply_convert_fusion.1 = bf16[2,12,512,512]{2,3,1,0:T(8,128)(2,1)S(1)} fusion(f32[2,12,512,512]{2,3,1,0:T(8,128)} %get-tuple-element.54, f32[2,12,512]{2,1,0:T(8,128)S(1)} %get-tuple-element.53, f32[2,12,512,512]{2,3,1,0:T(8,128)} %get-tuple-element.39, f32[2,12,512]{2,1,0:T(8,128)S(1)} %copy-done.30), kind=kLoop, calls=%fused_computation.7 | loop fusion | flops 25165824 | bytes 63012864 | tf_op jit(solution)/shard_map/convert_element_type | solution.py:36
  480.0 6.3 convolution_multiply_fusion
  489.9 10.6 %fusion.77 = f32[2,12,64,512]{3,2,1,0:T(8,128)} fusion(bf16[2,12,512,512]{2,3,1,0:T(8,128)(2,1)} %copy-done.1, bf16[2,512,3,12,64]{1,4,3,0,2:T(8,128)(2,1)} %bitcast.236), kind=kOutput, calls=%fused_computation.139 | convolution fusion | flops 805306368 | bytes 17301504 | tf_op jit(solution)/shard_map/bhts,bthe->bshe/dot_general | solution.py:38
  504.1 8.0 bitcast_dynamic-update-slice_fusion
  517.5 6.4 bitcast_dynamic-update-slice_fusion.1
  526.8 6.8 broadcast_multiply_fusion
  546.8 65.3 %psum.15 = f32[14592]{0:T(1024)S(1)} all-reduce(f32[14592]{0:T(1024)S(1)} %broadcast_multiply_fusion.1), channel_id=1, replica_groups=mesh['dp'=2,'fsdp'=64] {'fsdp','dp'}, use_global_device_ids=true, to_apply=%region_34.35 | all-reduce | flops 14592 | bytes 116736 | tf_op jit(solution)/shard_map/psum | solution.py:155
  612.7 9.9 %bitcast_convert_fusion = bf16[2,768,768]{2,1,0:T(8,128)(2,1)} fusion(bf16[2,768,768,1]{2,1,0,3:T(8,128)(2,1)} %bitcast.239, f32[2,768,1,768]{3,1,2,0:T(8,128)} %copy.59, f32[2,768,1,768]{3,1,2,0:T(8,128)} %copy.58), kind=kOutput, calls=%fused_computation.74 | convolution fusion | flops 3627417600 | bytes 14155776 | tf_op jit(solution)/shard_map/bsne,nde->bsd/dot_general | solution.py:111
  630.2 194.7 %reduce-scatter.3.cloned.1.call-done = f32[48,768]{1,0:T(8,128)} async-done(((f32[6144,768]{1,0:T(8,128)}), f32[48,768]{1,0:T(8,128)}) %reduce-scatter.3.cloned.1.call-update) | async-done | bytes 147472 | tf_op jit(solution)/shard_map/reduce_scatter | solution.py:151
  (212 shorter events, 111.9 us)
Async XLA Ops:
  7.2 128.9 %copy-start = (bf16[2,768,768]{2,1,0:T(8,128)(2,1)S(1)}, bf16[2,768,768]{2,1,0:T(8,128)(2,1)}, u32[]{:S(2)}) copy-start(bf16[2,768,768]{2,1,0:T(8,128)(2,1)} %param.10) | copy-start | bytes 7077892
  7.2 78.5 %all-gather.3.cloned.1.call-start = ((), (), s32[]{:S(2)}) async-start(), calls=%async_computation.2 | async-start | bytes 9510912 | tf_op jit(solution)/shard_map/all_gather | solution.py:142
  8.9 173.6 %all-gather.5.cloned.1.call-start = ((), (), s32[]{:S(2)}) async-start(), calls=%async_computation.3 | async-start | bytes 9510912 | tf_op jit(solution)/shard_map/all_gather | solution.py:142
  10.5 617.1 %reduce-scatter.5.cloned.1.call-start = ((), (), s32[]{:S(2)}) async-start(), calls=%async_computation.5 | async-start | bytes 19021824 | tf_op jit(solution)/shard_map/reduce_scatter | solution.py:151
  83.2 42.4 %copy-start.31 = (f32[768]{0:T(1024)}, f32[768]{0:T(1024)S(1)}, u32[]{:S(2)}) copy-start(f32[768]{0:T(1024)S(1)} %get-tuple-element.35) | copy-start | bytes 9220
  110.4 11.1 %copy-start.29 = (f32[2,12,512]{2,1,0:T(8,128)}, f32[2,12,512]{2,1,0:T(8,128)S(1)}, u32[]{:S(2)}) copy-start(f32[2,12,512]{2,1,0:T(8,128)S(1)} %get-tuple-element.38) | copy-start | bytes 147460
  110.4 11.1 %copy-start.50 = (bf16[2,512,768]{2,1,0:T(8,128)(2,1)S(1)}, bf16[2,512,768]{2,1,0:T(8,128)(2,1)}, u32[]{:S(2)}) copy-start(bf16[2,512,768]{2,1,0:T(8,128)(2,1)} %param.9) | copy-start | bytes 4718596
  160.8 14.9 %copy-start.22 = (bf16[2,512,768]{2,1,0:T(8,128)(2,1)S(1)}, bf16[2,512,768]{2,1,0:T(8,128)(2,1)}, u32[]{:S(2)}) copy-start(bf16[2,512,768]{2,1,0:T(8,128)(2,1)} %copy-done.21) | copy-start | bytes 4718596
  197.0 31.0 %copy-start.24 = (bf16[2,512,768]{2,1,0:T(8,128)(2,1)S(1)}, bf16[2,512,768]{2,1,0:T(8,128)(2,1)}, u32[]{:S(2)}) copy-start(bf16[2,512,768]{2,1,0:T(8,128)(2,1)} %add_convert_fusion.2) | copy-start | bytes 4718596
  197.0 31.0 %copy-start.46 = (f32[768]{0:T(1024)S(1)}, f32[768]{0:T(1024)}, u32[]{:S(2)}) copy-start(f32[768]{0:T(1024)} %get-tuple-element.30) | copy-start | bytes 9220
  235.6 37.1 %copy-start.6 = (f32[2,512,768]{2,1,0:T(8,128)}, f32[2,512,768]{2,1,0:T(8,128)S(1)}, u32[]{:S(2)}) copy-start(f32[2,512,768]{2,1,0:T(8,128)S(1)} %get-tuple-element.48) | copy-start | bytes 9437188
  235.7 37.1 %copy-start.27 = (f32[2,512]{1,0:T(2,128)}, f32[2,512]{1,0:T(2,128)S(1)}, u32[]{:S(2)}) copy-start(f32[2,512]{1,0:T(2,128)S(1)} %broadcast_multiply_fusion.8) | copy-start | bytes 12292
  236.2 36.6 %copy-start.37 = (f32[2,512]{1,0:T(2,128)}, f32[2,512]{1,0:T(2,128)S(1)}, u32[]{:S(2)}) copy-start(f32[2,512]{1,0:T(2,128)S(1)} %add_rsqrt_fusion) | copy-start | bytes 12292
  238.2 10.1 %slice-start.2 = ((s8[12582912]{0:T(1024)(128)(4,1)}), s8[4194304]{0:T(1024)(128)(4,1)S(1)}, s32[]{:S(2)}) async-start(s8[12582912]{0:T(1024)(128)(4,1)} %bitcast.218), calls=%async_computation.8 | async-start | bytes 8388608
  239.3 33.5 %copy-start.41 = (f32[2,512]{1,0:T(2,128)}, f32[2,512]{1,0:T(2,128)S(1)}, u32[]{:S(2)}) copy-start(f32[2,512]{1,0:T(2,128)S(1)} %get-tuple-element.57) | copy-start | bytes 12292
  239.3 33.5 %copy-start.43 = (f32[2,512]{1,0:T(2,128)}, f32[2,512]{1,0:T(2,128)S(1)}, u32[]{:S(2)}) copy-start(f32[2,512]{1,0:T(2,128)S(1)} %get-tuple-element.58) | copy-start | bytes 12292
  239.3 9.0 %slice-start.3 = ((s8[12582912]{0:T(1024)(128)(4,1)}), s8[4194304]{0:T(1024)(128)(4,1)S(1)}, s32[]{:S(2)}) async-start(s8[12582912]{0:T(1024)(128)(4,1)} %bitcast.218), calls=%async_computation.9 | async-start | bytes 8388608
  262.3 10.5 %copy-start.5 = (f32[2,512,768]{2,1,0:T(8,128)S(1)}, f32[2,512,768]{2,1,0:T(8,128)}, u32[]{:S(2)}) copy-start(f32[2,512,768]{2,1,0:T(8,128)} %copy-done.4) | copy-start | bytes 9437188
  262.3 10.5 %copy-start.54 = (bf16[2,512,3072]{2,1,0:T(8,128)(2,1)S(1)}, bf16[2,512,3072]{2,1,0:T(8,128)(2,1)}, u32[]{:S(2)}) copy-start(bf16[2,512,3072]{2,1,0:T(8,128)(2,1)} %get-tuple-element.56) | copy-start | bytes 18874372
  353.2 471.7 %reduce-scatter.3.cloned.1.call-start = ((), (), s32[]{:S(2)}) async-start(), calls=%async_computation.4 | async-start | bytes 19021824 | tf_op jit(solution)/shard_map/reduce_scatter | solution.py:151
  353.3 30.8 %copy-start.10 = (bf16[2,512,768]{1,2,0:T(8,128)(2,1)S(1)}, bf16[2,512,768]{1,2,0:T(8,128)(2,1)}, u32[]{:S(2)}) copy-start(bf16[2,512,768]{1,2,0:T(8,128)(2,1)} %copy.47) | copy-start | bytes 4718596
  402.0 10.6 %copy-start.3 = (f32[2,512,768]{2,1,0:T(8,128)S(1)}, f32[2,512,768]{2,1,0:T(8,128)}, u32[]{:S(2)}) copy-start(f32[2,512,768]{2,1,0:T(8,128)} %copy-done.2) | copy-start | bytes 9437188
  402.0 10.7 %copy-start.26 = (f32[2,512]{1,0:T(2,128)S(1)}, f32[2,512]{1,0:T(2,128)}, u32[]{:S(2)}) copy-start(f32[2,512]{1,0:T(2,128)} %copy-done.25) | copy-start | bytes 12292
  402.0 10.7 %copy-start.32 = (f32[768]{0:T(1024)S(1)}, f32[768]{0:T(1024)}, u32[]{:S(2)}) copy-start(f32[768]{0:T(1024)} %copy-done.31) | copy-start | bytes 9220
  402.0 10.7 %copy-start.34 = (f32[2,512]{1,0:T(2,128)S(1)}, f32[2,512]{1,0:T(2,128)}, u32[]{:S(2)}) copy-start(f32[2,512]{1,0:T(2,128)} %copy-done.33) | copy-start | bytes 12292
  500.5 17.0 %slice-start = ((s8[4718592]{0:T(1024)(128)(4,1)}), s8[524288]{0:T(1024)(128)(4,1)S(1)}, s32[]{:S(2)}) async-start(s8[4718592]{0:T(1024)(128)(4,1)} %bitcast.216), calls=%async_computation.6 | async-start | bytes 1048576
  504.1 13.4 %slice-start.1 = ((s8[4718592]{0:T(1024)(128)(4,1)}), s8[4194304]{0:T(1024)(128)(4,1)S(1)}, s32[]{:S(2)}) async-start(s8[4718592]{0:T(1024)(128)(4,1)} %bitcast.216), calls=%async_computation.7 | async-start | bytes 8388608
  612.7 9.9 %copy-start.7 = (f32[2,512,1,768]{3,1,2,0:T(8,128)S(1)}, f32[2,512,1,768]{3,1,2,0:T(8,128)}, u32[]{:S(2)}) copy-start(f32[2,512,1,768]{3,1,2,0:T(8,128)} %copy.57) | copy-start | bytes 9437188
  612.7 9.9 %copy-start.8 = (f32[2,512,1,768]{3,1,2,0:T(8,128)S(1)}, f32[2,512,1,768]{3,1,2,0:T(8,128)}, u32[]{:S(2)}) copy-start(f32[2,512,1,768]{3,1,2,0:T(8,128)} %copy.55) | copy-start | bytes 9437188
  612.7 9.9 %copy-start.9 = (f32[2,512,1,768]{3,1,2,0:T(8,128)S(1)}, f32[2,512,1,768]{3,1,2,0:T(8,128)}, u32[]{:S(2)}) copy-start(f32[2,512,1,768]{3,1,2,0:T(8,128)} %copy.56) | copy-start | bytes 9437188
  612.7 9.9 %copy-start.15 = (bf16[2304,768]{1,0:T(8,128)(2,1)S(1)}, bf16[2304,768]{1,0:T(8,128)(2,1)}, u32[]{:S(2)}) copy-start(bf16[2304,768]{1,0:T(8,128)(2,1)} %copy-done.14) | copy-start | bytes 10616836
  612.7 9.9 %copy-start.17 = (f32[2,512,768]{2,1,0:T(8,128)S(1)}, f32[2,512,768]{2,1,0:T(8,128)}, u32[]{:S(2)}) copy-start(f32[2,512,768]{2,1,0:T(8,128)} %copy-done.16) | copy-start | bytes 9437188
  (32 other events, 124.0 us)
Sparse Core Ops, SparseCore 0:
  11.6 74.0 all-gather.2
  89.3 68.0 all-gather.4
  353.4 232.2 reduce-scatter.4
  590.8 234.1 reduce-scatter.2

commit v2 on v1

v2 whole, which is shorter than its diff:
```python
import functools
import jax
import jax.numpy as jnp
from jax import lax
from jax.experimental import pallas as pl
from jax.experimental.pallas import tpu as pltpu
from jax.sharding import PartitionSpec as P

HEAD_DIM = 64
LN_EPS = 1e-5
MASK_FILL = -1e30
VMEM_BYTES = 60 * 1024 * 1024
F32 = jnp.float32
BF16 = jnp.bfloat16
GROUP = 256
PAIR = 128


def dot(lhs, rhs, contract=((1,), (0,))):
    return lax.dot_general(lhs, rhs, (contract, ((), ())), preferred_element_type=F32)


def dot_nt(lhs, rhs):
    return dot(lhs, rhs, ((1,), (1,)))


def dot_tn(lhs, rhs):
    return dot(lhs, rhs, ((0,), (0,)))


def norm_rows(resid, gain, shift):
    mean = jnp.mean(resid, axis=-1, keepdims=True)
    centred = resid - mean
    inv_std = lax.rsqrt(jnp.mean(centred * centred, axis=-1, keepdims=True) + LN_EPS)
    normed = centred * inv_std
    return (normed * gain + shift).astype(BF16), normed, inv_std


def norm_rows_bwd(d_out, normed, inv_std, gain):
    d_norm = d_out * gain
    return inv_std * (d_norm - jnp.mean(d_norm, axis=-1, keepdims=True) - normed * jnp.mean(d_norm * normed, axis=-1, keepdims=True))


def col_sum(values):
    return jnp.sum(values, axis=0, keepdims=True)


def head_masks(pair_q, pair_k, head, n_valid):
    lane_q = lax.broadcasted_iota(jnp.int32, pair_q.shape, 1)
    lane_k = lax.broadcasted_iota(jnp.int32, pair_k.shape, 1)
    row_k = lax.broadcasted_iota(jnp.int32, pair_k.shape, 0)
    spare = HEAD_DIM * (1 - head)
    own_q = (lane_q >= HEAD_DIM * head) & (lane_q < HEAD_DIM * (head + 1))
    own_k = (lane_k >= HEAD_DIM * head) & (lane_k < HEAD_DIM * (head + 1))
    q_f = jnp.where(own_q, pair_q.astype(F32), jnp.where(lane_q == spare, 1.0, 0.0)).astype(BF16)
    k_f = jnp.where(own_k, pair_k.astype(F32), jnp.where((lane_k == spare) & (row_k >= n_valid), MASK_FILL, 0.0)).astype(BF16)
    return q_f, k_f


def half_only(pair, head):
    lane = lax.broadcasted_iota(jnp.int32, pair.shape, 1)
    own = (lane >= HEAD_DIM * head) & (lane < HEAD_DIM * (head + 1))
    return jnp.where(own, pair.astype(F32), 0.0).astype(pair.dtype)


def join_halves(first, second):
    lane = lax.broadcasted_iota(jnp.int32, first.shape, 1)
    return jnp.where(lane < HEAD_DIM, first, second)


def scores_t(q_f, k_f, causal):
    s_t = dot_nt(k_f, q_f)
    if causal:
        key_i = lax.broadcasted_iota(jnp.int32, s_t.shape, 0)
        qry_i = lax.broadcasted_iota(jnp.int32, s_t.shape, 1)
        s_t = jnp.where(key_i <= qry_i, s_t, MASK_FILL)
    return s_t


def attend_group(q_g, k_g, v_g, n_valid, causal, lse_ref):
    o_parts = []
    for pair in range(GROUP // PAIR):
        cols = slice(pair * PAIR, (pair + 1) * PAIR)
        q2, k2, v2 = q_g[:, cols], k_g[:, cols], v_g[:, cols]
        v2_t = v2.T
        for head in range(2):
            q_f, k_f = head_masks(q2, k2, head, n_valid)
            s_t = scores_t(q_f, k_f, causal)
            top = jnp.max(s_t, axis=0, keepdims=True)
            e_t = jnp.exp(s_t - top)
            total = jnp.sum(e_t, axis=0, keepdims=True)
            p_t = (e_t * (1.0 / total)).astype(BF16)
            lse_ref[0, 0, pl.ds(2 * pair + head, 1), :] = top + jnp.log(total)
            o_parts.append(dot(v2_t[HEAD_DIM * head:HEAD_DIM * (head + 1)], p_t))
    return jnp.concatenate(o_parts, axis=0).T.astype(BF16)


def attend_group_bwd(d_o, q_g, k_g, v_g, n_valid, causal, lse_ref):
    dq_t, dk, dv = [], [], []
    for pair in range(GROUP // PAIR):
        cols = slice(pair * PAIR, (pair + 1) * PAIR)
        q2, k2, v2, do2 = q_g[:, cols], k_g[:, cols], v_g[:, cols], d_o[:, cols]
        k2_t = k2.T
        dk_h, dv_h = [], []
        for head in range(2):
            q_f, k_f = head_masks(q2, k2, head, n_valid)
            s_t = scores_t(q_f, k_f, causal)
            p_t = jnp.exp(s_t - lse_ref[0, 0, pl.ds(2 * pair + head, 1), :])
            dp_t = dot_nt(half_only(v2, head), do2)
            weighted = p_t * dp_t
            ds_t = (weighted - p_t * jnp.sum(weighted, axis=0, keepdims=True)).astype(BF16)
            dv_h.append(dot(p_t.astype(BF16), do2))
            dk_h.append(dot(ds_t, q2))
            dq_t.append(dot(k2_t[HEAD_DIM * head:HEAD_DIM * (head + 1)], ds_t))
        dk.append(join_halves(*dk_h))
        dv.append(join_halves(*dv_h))
    return jnp.concatenate(dq_t, axis=0).T * 0.125, jnp.concatenate(dk, axis=1), jnp.concatenate(dv, axis=1)


def attn_fwd_kernel(causal, slots, lens_ref, x_ref, kv_ref, wq_ref, wk_ref, wv_ref, wo_ref, bias_ref, rows_ref,
                    q_ref, k_ref, v_ref, o_ref, lse_ref, h_ref, normed_ref, inv_ref, acc_ref):
    q_row, k_row, v_row, o_row, gain_row = slots
    sample, group = pl.program_id(0), pl.program_id(1)
    x_b, kv_b = x_ref[...], kv_ref[...]
    q_g = ((dot(x_b, wq_ref[...]) + bias_ref[q_row:q_row + 1, :]) * 0.125).astype(BF16)
    k_g = (dot(kv_b, wk_ref[...]) + bias_ref[k_row:k_row + 1, :]).astype(BF16)
    v_g = (dot(kv_b, wv_ref[...]) + bias_ref[v_row:v_row + 1, :]).astype(BF16)
    q_ref[...], k_ref[...], v_ref[...] = q_g, k_g, v_g
    o_g = attend_group(q_g, k_g, v_g, lens_ref[sample], causal, lse_ref)
    o_ref[...] = o_g
    part = dot(o_g, wo_ref[...])

    @pl.when(group == 0)
    def _():
        acc_ref[...] = x_ref[...].astype(F32) + part

    @pl.when(group > 0)
    def _():
        acc_ref[...] += part

    @pl.when(group == pl.num_programs(1) - 1)
    def _():
        resid = acc_ref[...] + rows_ref[o_row:o_row + 1, :]
        h_out, normed, inv_std = norm_rows(resid, rows_ref[gain_row:gain_row + 1, :], rows_ref[gain_row + 1:gain_row + 2, :])
        h_ref[...], normed_ref[...], inv_ref[...] = h_out, normed, inv_std


def attn_forward(x, kv, lens, attn_full, bias_rows, mats, slots, causal):
    d_model = x.shape[-1]
    n_batch = lens.shape[0]
    n_q, n_k = x.shape[0] // n_batch, kv.shape[0] // n_batch
    n_groups = d_model // GROUP
    col = lambda mat: pl.BlockSpec((d_model, GROUP), lambda b, g: (mat, g))
    row = lambda mat: pl.BlockSpec((GROUP, d_model), lambda b, g: (mat * n_groups + g, 0))
    q_blk = pl.BlockSpec((n_q, GROUP), lambda b, g: (b, g))
    k_blk = pl.BlockSpec((n_k, GROUP), lambda b, g: (b, g))
    tok = lambda n: pl.BlockSpec((n, d_model), lambda b, g: (b, 0))
    n_heads_g = GROUP // HEAD_DIM
    out_shape = (
        jax.ShapeDtypeStruct(x.shape, BF16), jax.ShapeDtypeStruct(kv.shape, BF16), jax.ShapeDtypeStruct(kv.shape, BF16),
        jax.ShapeDtypeStruct(x.shape, BF16), jax.ShapeDtypeStruct((n_batch, n_groups, n_heads_g, n_q), F32),
        jax.ShapeDtypeStruct(x.shape, BF16), jax.ShapeDtypeStruct(x.shape, F32), jax.ShapeDtypeStruct((x.shape[0], 1), F32))
    return pl.pallas_call(
        functools.partial(attn_fwd_kernel, causal, slots),
        grid=(n_batch, n_groups),
        in_specs=[pl.BlockSpec(memory_space=pltpu.SMEM), tok(n_q), tok(n_k), col(mats[0]), col(mats[1]), col(mats[2]), row(mats[3]),
                  pl.BlockSpec((bias_rows.shape[0], GROUP), lambda b, g: (0, g)), pl.BlockSpec(bias_rows.shape, lambda b, g: (0, 0))],
        out_specs=[q_blk, k_blk, k_blk, q_blk, pl.BlockSpec((1, 1, n_heads_g, n_q), lambda b, g: (b, g, 0, 0)),
                   tok(n_q), tok(n_q), pl.BlockSpec((n_q, 1), lambda b, g: (b, 0))],
        out_shape=out_shape,
        scratch_shapes=[pltpu.VMEM((n_q, d_model), F32)],
        compiler_params=pltpu.CompilerParams(vmem_limit_bytes=VMEM_BYTES, dimension_semantics=('arbitrary', 'arbitrary')),
        cost_estimate=pl.CostEstimate(flops=2 * d_model * d_model * (2 * x.shape[0] + 2 * kv.shape[0]) + 16 * x.shape[0] * n_k * d_model, bytes_accessed=20 * x.shape[0] * d_model, transcendentals=0),
        name='attn_fwd',
    )(lens, x, kv, attn_full, attn_full, attn_full, attn_full, bias_rows, bias_rows)


def attn_bwd_kernel(causal, gain_row, lens_ref, dres_ref, wq_ref, wk_ref, wv_ref, wo_ref, q_ref, k_ref, v_ref, lse_ref,
                    rows_ref, normed_ref, inv_ref, dq_ref, dk_ref, dv_ref, dx_ref, dkv_ref, sums_ref, tail_ref, acc_ref, acc_kv_ref):
    sample, group = pl.program_id(0), pl.program_id(1)
    d_o = dot_nt(dres_ref[...].astype(BF16), wo_ref[...]).astype(BF16)
    dq, dk, dv = attend_group_bwd(d_o, q_ref[...], k_ref[...], v_ref[...], lens_ref[sample], causal, lse_ref)
    sums_ref[0, 0:1, :] = col_sum(dq)
    sums_ref[0, 1:2, :] = col_sum(dk)
    sums_ref[0, 2:3, :] = col_sum(dv)
    dq_b, dk_b, dv_b = dq.astype(BF16), dk.astype(BF16), dv.astype(BF16)
    dq_ref[...], dk_ref[...], dv_ref[...] = dq_b, dk_b, dv_b
    part_q = dot_nt(dq_b, wq_ref[...])
    part_kv = dot_nt(dk_b, wk_ref[...]) + dot_nt(dv_b, wv_ref[...])
    last = pl.num_programs(1) - 1
    if causal:
        @pl.when(group == 0)
        def _():
            acc_ref[...] = dres_ref[...] + part_q + part_kv

        @pl.when(group > 0)
        def _():
            acc_ref[...] += part_q + part_kv

        @pl.when(group == last)
        def _():
            dx_ref[...] = acc_ref[...].astype(BF16)
            tail_ref[...] = jnp.zeros_like(tail_ref)
    else:
        @pl.when(group == 0)
        def _():
            acc_ref[...] = dres_ref[...] + part_q
            acc_kv_ref[...] = part_kv

        @pl.when(group > 0)
        def _():
            acc_ref[...] += part_q
            acc_kv_ref[...] += part_kv

        @pl.when(group == last)
        def _():
            d_h = acc_ref[...]
            normed = normed_ref[...]
            d_resid = norm_rows_bwd(d_h, normed, inv_ref[...], rows_ref[gain_row:gain_row + 1, :])
            dx_ref[...] = d_resid
            dkv_ref[...] = acc_kv_ref[...].astype(BF16)
            tail_ref[0, 0:1, :] = col_sum(d_resid)
            tail_ref[0, 1:2, :] = col_sum(d_h * normed)
            tail_ref[0, 2:3, :] = col_sum(d_h)


def attn_backward(dres, q, k, v, lse, lens, attn_full, bias_rows, mats, causal, gain_row=0, normed=None, inv_std=None):
    d_model = q.shape[-1]
    n_batch = lens.shape[0]
    n_q, n_k = q.shape[0] // n_batch, k.shape[0] // n_batch
    n_groups = d_model // GROUP
    col = lambda mat: pl.BlockSpec((d_model, GROUP), lambda b, g: (mat, g))
    row = lambda mat: pl.BlockSpec((GROUP, d_model), lambda b, g: (mat * n_groups + g, 0))
    q_blk = pl.BlockSpec((n_q, GROUP), lambda b, g: (b, g))
    k_blk = pl.BlockSpec((n_k, GROUP), lambda b, g: (b, g))
    tok = lambda n: pl.BlockSpec((n, d_model), lambda b, g: (b, 0))
    n_heads_g = GROUP // HEAD_DIM
    whole_rows = pl.BlockSpec(bias_rows.shape, lambda b, g: (0, 0))
    kernel = functools.partial(attn_bwd_kernel, causal, gain_row)
    in_specs = [pl.BlockSpec(memory_space=pltpu.SMEM), tok(n_q), col(mats[0]), col(mats[1]), col(mats[2]), row(mats[3]), q_blk, k_blk, k_blk,
                pl.BlockSpec((1, 1, n_heads_g, n_q), lambda b, g: (b, g, 0, 0)), whole_rows]
    args = [lens, dres, attn_full, attn_full, attn_full, attn_full, q, k, v, lse, bias_rows]
    sums_blk = pl.BlockSpec((1, 8, GROUP), lambda b, g: (b, 0, g))
    tail_blk = pl.BlockSpec((1, 8, d_model), lambda b, g: (b, 0, 0))
    tail_shape = jax.ShapeDtypeStruct((n_batch, 8, d_model), F32)
    out_shape = [jax.ShapeDtypeStruct(q.shape, BF16), jax.ShapeDtypeStruct(k.shape, BF16), jax.ShapeDtypeStruct(k.shape, BF16),
                 jax.ShapeDtypeStruct(q.shape, BF16 if causal else F32)]
    out_specs = [q_blk, k_blk, k_blk, tok(n_q)]
    scratch = [pltpu.VMEM((n_q, d_model), F32)]
    if causal:
        def body(*refs):
            ins, rest = refs[:11], refs[11:]
            dq, dk, dv, dx, sums, tail, acc = rest
            kernel(*ins, None, None, dq, dk, dv, dx, None, sums, tail, acc, None)
    else:
        in_specs += [tok(n_q), pl.BlockSpec((n_q, 1), lambda b, g: (b, 0))]
        args += [normed, inv_std]
        out_shape.append(jax.ShapeDtypeStruct(k.shape, BF16))
        out_specs.append(tok(n_k))
        scratch.append(pltpu.VMEM((n_k, d_model), F32))
        body = kernel
    out_shape += [tail_shape, tail_shape]
    out_specs += [sums_blk, tail_blk]
    return pl.pallas_call(
        body, grid=(n_batch, n_groups), in_specs=in_specs, out_specs=out_specs, out_shape=out_shape, scratch_shapes=scratch,
        compiler_params=pltpu.CompilerParams(vmem_limit_bytes=VMEM_BYTES, dimension_semantics=('arbitrary', 'arbitrary')),
        cost_estimate=pl.CostEstimate(flops=2 * d_model * d_model * (2 * q.shape[0] + 2 * k.shape[0]) + 40 * q.shape[0] * n_k * d_model, bytes_accessed=20 * q.shape[0] * d_model, transcendentals=0),
        name='attn_bwd',
    )(*args)


def ffn_kernel(h_ref, dy_ref, up_ref, down_ref, rows_ref, bias_ref, normed_ref, inv_ref,
               y_ref, gelu_ref, dup_ref, dres3_ref, dres2_ref, tail_ref, upsum_ref):
    step = pl.program_id(0)
    h_b = h_ref[...]
    up = dot_nt(h_b, up_ref[...]) + bias_ref[...]
    cdf = 0.5 * (1.0 + lax.erf(up * 0.7071067811865476))
    gelu = (up * cdf).astype(BF16)
    slope = cdf + up * (0.3989422804014327 * jnp.exp(-0.5 * up * up))
    gelu_ref[...] = gelu
    resid = h_b.astype(F32) + dot(gelu, down_ref[...]) + rows_ref[8:9, :]
    y_b, normed3, inv3 = norm_rows(resid, rows_ref[13:14, :], rows_ref[14:15, :])
    y_ref[...] = y_b
    dy = dy_ref[...].astype(F32)
    d_res3 = norm_rows_bwd(dy, normed3, inv3, rows_ref[13:14, :])
    d_res3_b = d_res3.astype(BF16)
    dres3_ref[...] = d_res3_b
    d_up = dot_nt(d_res3_b, down_ref[...]) * slope
    d_up_b = d_up.astype(BF16)
    dup_ref[...] = d_up_b
    d_h2 = d_res3 + dot(d_up_b, up_ref[...])
    normed2 = normed_ref[...]
    d_res2 = norm_rows_bwd(d_h2, normed2, inv_ref[...], rows_ref[11:12, :])
    dres2_ref[...] = d_res2
    tail = jnp.concatenate([col_sum(d_res2), col_sum(d_res3), col_sum(d_h2 * normed2), col_sum(d_h2), col_sum(dy * normed3), col_sum(dy),
                            jnp.zeros((2, dy.shape[1]), F32)], axis=0)
    up_sum = col_sum(d_up)

    @pl.when(step == 0)
    def _():
        tail_ref[...] = tail
        upsum_ref[...] = up_sum

    @pl.when(step > 0)
    def _():
        tail_ref[...] += tail
        upsum_ref[...] += up_sum


def ffn_both(h2, dy, ffn_full, bias_rows, up_bias, normed2, inv2, block=256):
    n_tok, d_model = h2.shape
    ffn_dim = ffn_full.shape[0] // 2
    tok = pl.BlockSpec((block, d_model), lambda i: (i, 0))
    wide = pl.BlockSpec((block, ffn_dim), lambda i: (i, 0))
    once = lambda shape, idx: pl.BlockSpec(shape, lambda i: idx, pipeline_mode=pl.Buffered(1))
    return pl.pallas_call(
        ffn_kernel, grid=(n_tok // block,),
        in_specs=[tok, tok, once((ffn_dim, d_model), (0, 0)), once((ffn_dim, d_model), (1, 0)), once(bias_rows.shape, (0, 0)), once((1, ffn_dim), (0, 0)),
                  tok, pl.BlockSpec((block, 1), lambda i: (i, 0))],
        out_specs=[tok, wide, wide, tok, tok, pl.BlockSpec((8, d_model), lambda i: (0, 0)), pl.BlockSpec((1, ffn_dim), lambda i: (0, 0))],
        out_shape=[jax.ShapeDtypeStruct(h2.shape, BF16), jax.ShapeDtypeStruct((n_tok, ffn_dim), BF16), jax.ShapeDtypeStruct((n_tok, ffn_dim), BF16),
                   jax.ShapeDtypeStruct(h2.shape, BF16), jax.ShapeDtypeStruct(h2.shape, F32),
                   jax.ShapeDtypeStruct((8, d_model), F32), jax.ShapeDtypeStruct((1, ffn_dim), F32)],
        compiler_params=pltpu.CompilerParams(vmem_limit_bytes=VMEM_BYTES, dimension_semantics=('arbitrary',)),
        cost_estimate=pl.CostEstimate(flops=8 * n_tok * d_model * ffn_dim, bytes_accessed=30 * n_tok * d_model, transcendentals=0),
        name='ffn_both',
    )(h2, dy, ffn_full, ffn_full, bias_rows, up_bias, normed2, inv2)


def layer_acts(dec_in, enc_out, src_lens, tgt_lens, y_cot, attn_full, ffn_full, vec_full):
    n_batch, n_tgt, d_model = dec_in.shape
    x = dec_in.reshape(-1, d_model)
    enc = enc_out.reshape(-1, d_model)
    dy = y_cot.reshape(-1, d_model)
    vec_f = vec_full.astype(F32)
    bias_rows = jnp.pad(vec_f[:15 * d_model].reshape(15, d_model), ((0, 1), (0, 0)))
    up_bias = vec_f[15 * d_model:].reshape(1, -1)
    q1, k1, v1, o1, lse1, h1, normed1, inv1 = attn_forward(x, x, tgt_lens, attn_full, bias_rows, (0, 1, 2, 3), (0, 1, 2, 3, 9), True)
    q2, k2, v2, o2, lse2, h2, normed2, inv2 = attn_forward(h1, enc, src_lens, attn_full, bias_rows, (4, 5, 6, 7), (4, 5, 6, 7, 11), False)
    y, gelu, d_up, d_res3, d_res2, ffn_tail, up_sum = ffn_both(h2, dy, ffn_full, bias_rows, up_bias, normed2, inv2)
    dq2, dk2, dv2, d_res1, d_enc, sums2, tail2 = attn_backward(d_res2, q2, k2, v2, lse2, src_lens, attn_full, bias_rows, (4, 5, 6, 7), False, 9, normed1, inv1)
    dq1, dk1, dv1, d_x, sums1, _ = attn_backward(d_res1, q1, k1, v1, lse1, tgt_lens, attn_full, bias_rows, (0, 1, 2, 3), True)
    s1, s2, t2 = jnp.sum(sums1, axis=0), jnp.sum(sums2, axis=0), jnp.sum(tail2, axis=0)
    g_vec = jnp.concatenate([s1[0:3].reshape(-1), t2[0], s2[0:3].reshape(-1), ffn_tail[0], ffn_tail[1], t2[1], t2[2], ffn_tail[2], ffn_tail[3], ffn_tail[4], ffn_tail[5], up_sum[0]])
    pairs = ((x, dq1), (x, dk1), (x, dv1), (o1, d_res1.astype(BF16)), (h1, dq2), (enc, dk2), (enc, dv2), (o2, d_res2.astype(BF16)))
    ffn_pairs = ((d_up, h2), (gelu, d_res3))
    return y.reshape(dec_in.shape), d_x.reshape(dec_in.shape), d_enc.reshape(enc_out.shape), pairs, ffn_pairs, g_vec


def solution(mesh):
    n_fsdp = mesh.shape['fsdp']
    n_dp = mesh.shape['dp']
    batch_axes = ('dp', 'fsdp')
    all_axes = ('fsdp', 'dp')
    act_spec = P(batch_axes, None, None)
    len_spec = P(batch_axes)
    row_spec = P('fsdp', None)
    vec_spec = P('fsdp')

    def gather_rows(w_rows):
        half = w_rows.shape[0] // n_dp
        mine = lax.dynamic_slice_in_dim(w_rows, lax.axis_index('dp') * half, half, 0)
        return lax.all_gather(mine, all_axes, axis=0, tiled=True)

    def gather_vec(vec_rows):
        n_own = vec_rows.shape[0]
        mine = jnp.where(lax.axis_index('dp') == 0, vec_rows, jnp.zeros_like(vec_rows))
        full = lax.dynamic_update_slice_in_dim(jnp.zeros((n_own * n_fsdp,), vec_rows.dtype), mine, lax.axis_index('fsdp') * n_own, 0)
        return lax.psum(full, all_axes)

    def scatter_rows(full_grad):
        return lax.all_gather(lax.psum_scatter(full_grad, all_axes, scatter_dimension=0, tiled=True), 'dp', axis=0, tiled=True)

    def scatter_vec(full_grad):
        n_own = full_grad.shape[0] // n_fsdp
        return lax.dynamic_slice_in_dim(lax.psum(full_grad, all_axes), lax.axis_index('fsdp') * n_own, n_own, 0)

    def device_step(dec_in, enc_out, src_lens, tgt_lens, y_cot, attn_w, ffn_w, vec_params):
        y_out, dec_grad, enc_grad, pairs, ffn_pairs, g_vec = layer_acts(dec_in, enc_out, src_lens, tgt_lens, y_cot, gather_rows(attn_w), gather_rows(ffn_w), gather_vec(vec_params))
        grad_scale = 1.0 / (dec_in.shape[0] * dec_in.shape[1] * n_fsdp * n_dp)
        g_ffn = jnp.concatenate([dot_tn(lhs, rhs) for lhs, rhs in ffn_pairs], axis=0) * grad_scale
        g_attn = jnp.concatenate([dot_tn(lhs, rhs) for lhs, rhs in pairs], axis=0) * grad_scale
        return y_out, dec_grad, enc_grad, scatter_rows(g_attn), scatter_rows(g_ffn), scatter_vec(g_vec * grad_scale)

    return jax.shard_map(device_step, mesh=mesh, in_specs=(act_spec, act_spec, len_spec, len_spec, act_spec, row_spec, row_spec, vec_spec), out_specs=(act_spec, act_spec, act_spec, row_spec, row_spec, vec_spec), check_vma=False)
```

time: 845 us -> 705 us (0.83)
  matrix products: 312 us -> 27.9 us
  Pallas kernels: 0 us -> 166 us
  waiting for transfers between devices: 197 us -> 319 us
  other arithmetic: 122 us -> 17.2 us
  local copies, waits for them, and re-layouts: 49.8 us -> 9.92 us
    dot_general x31 -> x10, matrix products: 278 us -> 27.9 us  [dot(): lax.dot_general(lhs, rhs, (contract, ((), ())), preferred_element_type=F32)]
    pallas_call x0 -> x5, Pallas kernels: none -> 166 us  [the longest x2 75.7 us: attn_backward(): pl.pallas_call(body, grid=(n_batch, n_groups), in_specs=in_specs, out_spe...]
    reduce_scatter x2, waiting for transfers between devices: 195 us -> 301 us  [scatter_rows(): lax.psum_scatter(full_grad, all_axes, scatter_dimension=0, tiled=True)]
    convert_element_type x5 -> x0, other arithmetic: 80.9 us -> none  [the longest x2 47.6 us: attn_bwd(): (attn_prob * (d_prob - jnp.sum(attn_prob * d_prob, axis=-1, keepdims=True...]
    sub x2 -> x0, matrix products: 33.8 us -> none  [attn_fwd(): attn_prob = jax.nn.softmax(scores, axis=-1)]
    another operation x5 -> x0, local copies, waits for them, and re-layouts: 23 us -> none  [the longest x2 12.2 us: layer_backward(): jnp.stack([dk_cross, dv_cross], axis=2).reshape(n_batch, n_src, 2, d_model)]
    reduce_sum x9 -> x3, other arithmetic: 17.9 us -> 0.02 us  [the longest x1 0.01 us: layer_acts(): jnp.sum(tail2, axis=0)]
    all_gather x2, waiting for transfers between devices: 2.19 us -> 17.8 us  [gather_rows(): return lax.all_gather(mine, all_axes, axis=0, tiled=True)]
  transfers between devices with their start and end apart: 4 -> 4, of which waited for: 2 -> 4; matrix products, arithmetic and copies ran while one was open for 36% -> 4% of each run, Pallas kernels for 0% -> 19%
where the time goes in v2:
time: 705 us; the launch traced here: 698 us
  waiting for transfers between devices  319 us (45%)
  Pallas kernels  166 us (24%)
  blocking collectives  143 us (20%)
  matrix products  27.9 us (4%)
  other arithmetic  17.2 us (2%)
  between operations  14.7 us (2%)
  local copies, waits for them, and re-layouts  9.92 us (1%)
    reduce_scatter x2, waiting for transfers between devices, scatter_rows(): lax.psum_scatter(full_grad, all_axes, scatter_dimension=0, tiled=True)  301 us
    pallas_call x2, Pallas kernels, attn_backward(): pl.pallas_call(body, grid=(n_batch, n_groups), in_specs=in_specs, out_spe...  75.7 us
    psum x1, blocking collectives, gather_vec(): return lax.psum(full, all_axes)  70.2 us
    psum x1, blocking collectives, scatter_vec(): lax.psum(full_grad, all_axes)  64.5 us
    pallas_call x2, Pallas kernels, attn_forward(): pl.pallas_call(functools.partial(attn_fwd_kernel, causal, slots), grid=(n...  57.6 us
    pallas_call x1, Pallas kernels, ffn_both(): pl.pallas_call(ffn_kernel, grid=(n_tok // block,), in_specs=[tok, tok, on...  32.4 us
    dot_general x10, matrix products, dot(): lax.dot_general(lhs, rhs, (contract, ((), ())), preferred_element_type=F32)  27.9 us
    all_gather x2, waiting for transfers between devices, gather_rows(): return lax.all_gather(mine, all_axes, axis=0, tiled=True)  17.8 us
  transfers between devices with their start and end apart: 4, of which 4 were waited for; matrix products, arithmetic and copies ran while one was open for 4% of the time, Pallas kernels for 19%

profile of v2, /device:TPU:1, one launch (start us, length us, event | category | flops | bytes accessed | tf_op | source)
XLA Modules:
  0.0 697.6 jit_solution(18005083767917755571)
XLA Ops:
  7.2 0.9 copy-done
  8.1 0.6 constant_dynamic-slice_fusion.1
  8.8 1.5 constant_dynamic-slice_fusion
  10.7 70.2 %psum.14 = bf16[14592]{0:T(1024)(128)(2,1)S(1)} all-reduce(bf16[14592]{0:T(1024)(128)(2,1)S(1)} %dynamic_update_slice.3), channel_id=1, replica_groups=mesh['dp'=2,'fsdp'=64] {'fsdp','dp'}, use_global_device_ids=true, to_apply=%region_0.1 | all-reduce | flops 14592 | bytes 58368 | tf_op jit(solution)/shard_map/psum | solution.py:369
  82.1 3.7 all-gather.3.cloned.1.call-done.wq_ref.wk_ref.wv_ref.wo_ref.refs_2_.refs_3_.refs_4_.refs_5_
  85.8 25.7 %attn_fwd.2 = (bf16[1024,768]{1,0:T(8,128)(2,1)}, bf16[1024,768]{1,0:T(8,128)(2,1)}, bf16[1024,768]{1,0:T(8,128)(2,1)}, bf16[1024,768]{1,0:T(8,128)(2,1)}, f32[2...) custom-call(s32[2]{0:T(128)} %refs_0_.1, ...), custom_call_target="tpu_custom_call" | custom-call | flops 11274289152 | bytes 15728640 | tf_op jit(solution)/shard_map/attn_fwd/pallas_call | solution.py:163
  111.5 31.9 %attn_fwd.3 = (bf16[1024,768]{1,0:T(8,128)(2,1)}, bf16[1536,768]{1,0:T(8,128)(2,1)}, bf16[1536,768]{1,0:T(8,128)(2,1)}, bf16[1024,768]{1,0:T(8,128)(2,1)}, f32[2...) custom-call(s32[2]{0:T(128)} %lens_ref.5, ...), custom_call_target="tpu_custom_call" | custom-call | flops 15703474176 | bytes 15728640 | tf_op jit(solution)/shard_map/attn_fwd/pallas_call | solution.py:163
  143.5 14.1 %all-gather.5.cloned.1.call-done.up_ref.down_ref = bf16[6144,768]{1,0:T(8,128)(2,1)} async-done(((bf16[48,768]{1,0:T(8,128)(2,1)}), bf16[6144,768]{1,0:T(8,128)(2,1)}) %all-gather.5.cloned.1.call-update) | async-done | bytes 9437200 | tf_op jit(solution)/shard_map/all_gather | solution.py:363
  157.6 32.4 %ffn_both.1 = (bf16[1024,768]{1,0:T(8,128)(2,1)}, bf16[1024,3072]{1,0:T(8,128)(2,1)}, bf16[1024,3072]{1,0:T(8,128)(2,1)}, bf16[1024,768]{1,0:T(8,128)(2,1)}, f32...) custom-call(bf16[1024,768]{1,0:T(8,128)(2,1)} %get-tuple-element.42.h_ref, bf16[1024,768]{1,0:T(8,128)(2,1)} %bitcast.41, ...), custom_call_target="tpu_custom_call" | custom-call | flops 19327352832 | bytes 23592960 | tf_op jit(solution)/shard_map/ffn_both/pallas_call | solution.py:316
  190.0 7.8 %fusion.2 = f32[3072,768]{1,0:T(8,128)S(1)} fusion(bf16[1024,3072]{1,0:T(8,128)(2,1)} %get-tuple-element.68, bf16[1024,768]{1,0:T(8,128)(2,1)S(1)} %copy-done.20), kind=kOutput, calls=%fused_computation.37 | convolution fusion | flops 4831838208 | bytes 17301504 | tf_op jit(solution)/shard_map/dot_general | solution.py:20
  197.8 5.2 fusion.3
  203.0 10.4 %maximum_multiply_fusion = f32[6144,768]{1,0:T(8,128)} fusion(f32[3072,768]{1,0:T(8,128)S(1)} %fusion.3, f32[3072,768]{1,0:T(8,128)S(1)} %fusion.2), kind=kLoop, calls=%fused_computation | loop fusion | flops 9437184 | bytes 37748736 | tf_op jit(solution)/shard_map/mul | solution.py:381
  213.5 44.3 %attn_bwd.2 = (bf16[1024,768]{1,0:T(8,128)(2,1)}, bf16[1536,768]{1,0:T(8,128)(2,1)}, bf16[1536,768]{1,0:T(8,128)(2,1)}, f32[1024,768]{1,0:T(8,128)}, bf16[1536,7...) custom-call(s32[2]{0:T(128)} %lens_ref.5, f32[1024,768]{1,0:T(8,128)} %get-tuple-element.46.dres_ref, ...), custom_call_target="tpu_custom_call" | custom-call | flops 30198988800 | bytes 15728640 | tf_op jit(solution)/shard_map/attn_bwd/pallas_call | solution.py:264
  257.8 31.4 %attn_bwd.3 = (bf16[1024,768]{1,0:T(8,128)(2,1)}, bf16[1024,768]{1,0:T(8,128)(2,1)}, bf16[1024,768]{1,0:T(8,128)(2,1)}, bf16[1024,768]{1,0:T(8,128)(2,1)}, f32[2,8,768]{2,1,0:T(8,128)}, /*index=5*/f32[2,8,768]{2,1,0:T(8,128)}) custom-call(s32[2]{0:T(128)} %refs_0_.1, f32[1024,768]{1,0:T(8,128)} %get-tuple-element.53.refs_1_, ...), custom_call_target="tpu_custom_call" | custom-call | flops 20937965568 | bytes 15728640 | tf_op jit(solution)/shard_map/attn_bwd/pallas_call | solution.py:264
  289.2 3.0 bitcast_dynamic-update-slice_fusion.4
  292.2 1.5 bitcast_dynamic-update-slice_fusion.3
  293.7 1.5 bitcast_dynamic-update-slice_fusion.2
  296.1 1.5 convolution_dynamic-update-slice_fusion.2
  298.0 1.5 convolution_dynamic-update-slice_fusion.1
  299.6 0.7 copy-done.18
  300.3 2.1 bitcast_dynamic-update-slice_fusion.1
  302.5 2.1 bitcast_dynamic-update-slice_fusion
  304.9 1.7 convolution_dynamic-update-slice_fusion
  306.6 6.8 broadcast_multiply_fusion
  313.5 0.7 copy-done.3
  314.6 64.5 %psum.15 = f32[14592]{0:T(1024)S(1)} all-reduce(f32[14592]{0:T(1024)S(1)} %broadcast_multiply_fusion.1), channel_id=1, replica_groups=mesh['dp'=2,'fsdp'=64] {'fsdp','dp'}, use_global_device_ids=true, to_apply=%region_6.7 | all-reduce | flops 14592 | bytes 116736 | tf_op jit(solution)/shard_map/psum | solution.py:376
  379.7 66.2 %reduce-scatter.5.cloned.1.call-done = f32[48,768]{1,0:T(8,128)} async-done(((f32[6144,768]{1,0:T(8,128)}), f32[48,768]{1,0:T(8,128)}) %reduce-scatter.5.cloned.1.call-update) | async-done | bytes 147472 | tf_op jit(solution)/shard_map/reduce_scatter | solution.py:372
  445.9 4.3 all_gather.15
  450.2 234.7 %reduce-scatter.3.cloned.1.call-done = f32[48,768]{1,0:T(8,128)} async-done(((f32[6144,768]{1,0:T(8,128)}), f32[48,768]{1,0:T(8,128)}) %reduce-scatter.3.cloned.1.call-update) | async-done | bytes 147472 | tf_op jit(solution)/shard_map/reduce_scatter | solution.py:372
  685.0 4.3 all_gather.14
  689.2 0.7 copy.36
  690.0 0.7 copy.37
  (80 shorter events, 4.3 us)
Async XLA Ops:
  7.2 0.9 copy-start
  7.2 78.7 %all-gather.3.cloned.1.call-start = ((), (), s32[]{:S(2)}) async-start(), calls=%async_computation.2 | async-start | bytes 9510912 | tf_op jit(solution)/shard_map/all_gather | solution.py:363
  8.7 148.8 %all-gather.5.cloned.1.call-start = ((), (), s32[]{:S(2)}) async-start(), calls=%async_computation.3 | async-start | bytes 9510912 | tf_op jit(solution)/shard_map/all_gather | solution.py:363
  10.4 435.6 %reduce-scatter.5.cloned.1.call-start = ((), (), s32[]{:S(2)}) async-start(), calls=%async_computation.5 | async-start | bytes 19021824 | tf_op jit(solution)/shard_map/reduce_scatter | solution.py:372
  157.6 32.4 %copy-start.20 = (bf16[1024,768]{1,0:T(8,128)(2,1)S(1)}, bf16[1024,768]{1,0:T(8,128)(2,1)}, u32[]{:S(2)}) copy-start(bf16[1024,768]{1,0:T(8,128)(2,1)} %get-tuple-element.42.h_ref) | copy-start | bytes 4718596
  189.9 7.8 %copy-start.19 = (bf16[1024,3072]{1,0:T(8,128)(2,1)S(1)}, bf16[1024,3072]{1,0:T(8,128)(2,1)}, u32[]{:S(2)}) copy-start(bf16[1024,3072]{1,0:T(8,128)(2,1)} %get-tuple-element.69) | copy-start | bytes 18874372
  189.9 7.8 %copy-start.21 = (bf16[1024,768]{1,0:T(8,128)(2,1)S(1)}, bf16[1024,768]{1,0:T(8,128)(2,1)}, u32[]{:S(2)}) copy-start(bf16[1024,768]{1,0:T(8,128)(2,1)} %get-tuple-element.70) | copy-start | bytes 4718596
  213.4 471.5 %reduce-scatter.3.cloned.1.call-start = ((), (), s32[]{:S(2)}) async-start(), calls=%async_computation.4 | async-start | bytes 19021824 | tf_op jit(solution)/shard_map/reduce_scatter | solution.py:372
  257.7 31.5 %copy-start.8 = (bf16[2,512,768]{2,1,0:T(8,128)(2,1)S(1)}, bf16[2,512,768]{2,1,0:T(8,128)(2,1)}, u32[]{:S(2)}) copy-start(bf16[2,512,768]{2,1,0:T(8,128)(2,1)} %param.8) | copy-start | bytes 4718596
  289.2 3.0 copy-start.16
  292.2 1.5 copy-start.15
  293.7 1.9 copy-start.10
  293.7 2.3 copy-start.12
  296.1 1.5 copy-start.11
  296.1 1.9 copy-start.14
  298.0 1.7 copy-start.7
  298.0 2.4 copy-start.18
  300.3 2.2 copy-start.17
  302.5 2.2 copy-start.9
  302.5 2.3 copy-start.13
  313.4 0.8 copy-start.3
  313.4 0.8 copy-start.2
  313.4 0.8 copy-start.4
  313.4 1.0 copy-start.5
  313.4 1.1 copy-start.6
  313.4 377.2 %copy-start.1 = (bf16[96,768]{1,0:T(8,128)(2,1)S(1)}, bf16[96,768]{1,0:T(8,128)(2,1)}, u32[]{:S(2)}) copy-start(bf16[96,768]{1,0:T(8,128)(2,1)} %param.13) | copy-start | bytes 442372
Sparse Core Ops, SparseCore 0:
  11.6 74.1 all-gather.2
  89.4 68.0 all-gather.4
  213.5 232.3 reduce-scatter.4
  451.1 233.8 reduce-scatter.2

commit v3 on v2

--- a/solution.py
+++ b/solution.py
@@ -345,6 +345,292 @@
     pairs = ((x, dq1), (x, dk1), (x, dv1), (o1, d_res1.astype(BF16)), (h1, dq2), (enc, dk2), (enc, dv2), (o2, d_res2.astype(BF16)))
     ffn_pairs = ((d_up, h2), (gelu, d_res3))
     return y.reshape(dec_in.shape), d_x.reshape(dec_in.shape), d_enc.reshape(enc_out.shape), pairs, ffn_pairs, g_vec
+SIDE = 4
+LANES = 128
+COLOURS = 3
+DIM_ORDER = ((2, 1, 0), (1, 0, 2), (0, 2, 1))
+MESH_ID = pl.DeviceIdType.MESH
+
+
+def torus_place():
+    chip = lax.axis_index('fsdp')
+    return (chip // (SIDE * SIDE), (chip // SIDE) % SIDE, chip % SIDE)
+
+
+def chip_at(place, dim, shift):
+    moved = [lax.rem(p + shift + SIDE, SIDE) if d == dim else p for d, p in enumerate(place)]
+    return (moved[0] * SIDE + moved[1]) * SIDE + moved[2]
+
+
+def meet_neighbours(place):
+    barrier = pltpu.get_barrier_semaphore()
+    core = lax.axis_index('dp')
+    for dim in range(3):
+        for shift in (1, -1):
+            pl.semaphore_signal(barrier, inc=1, device_id=(core, chip_at(place, dim, shift)), device_id_type=MESH_ID)
+    pl.semaphore_signal(barrier, inc=1, device_id=(1 - core, lax.axis_index('fsdp')), device_id_type=MESH_ID)
+    pl.semaphore_wait(barrier, 7)
+
+
+class Counter:
+    def __init__(self):
+        self.used = 0
+
+    def take(self):
+        self.used += 1
+        return self.used - 1
+
+
+def rs_kernel(scale, rows, vec_rows, gffn_ref, gattn_ref, gvec_ref, offn_ref, oattn_ref, ovec_ref,
+              acc0, acc1, g10, g11, d10, d11, g20, g21, d20, d21, g30, g31, d30, d31, stage, send_sem, recv_sem, load_sem):
+    core = lax.axis_index('dp')
+    chip = lax.axis_index('fsdp')
+    place = torus_place()
+    acc = (acc0, acc1)
+    got = ((g10, g20, g30), (g11, g21, g31))
+    far = ((d10, d20, d30), (d11, d21, d31))
+    height = (rows, rows + vec_rows)
+    counter = Counter()
+    started = []
+
+    def remote(src, dst, device):
+        i = counter.take()
+        return pltpu.make_async_remote_copy(src_ref=src, dst_ref=dst, send_sem=send_sem.at[i], recv_sem=recv_sem.at[i], device_id=device, device_id_type=MESH_ID)
+
+    def start(copy):
+        copy.start()
+        started.append(copy)
+
+    sibling = (1 - core, chip)
+
+    def columns(of_core, colour):
+        return pl.ds(pl.multiple_of((of_core * COLOURS + colour) * LANES, LANES), LANES)
+
+    def slot(colour, d):
+        dim = DIM_ORDER[colour][0]
+        where = [slice(None)] * 3
+        where[dim] = lax.rem(place[dim] + d, SIDE)
+        return tuple(where)
+
+    pieces = [(q, d, colour) for q in range(2) for d in (2, 1, 3, 0) for colour in range(COLOURS)]
+    sources = (gffn_ref, gattn_ref)
+
+    def swap_copies(q, d, colour):
+        where = slot(colour, d)
+        cols = columns(1 - core, colour)
+        copies = [remote(sources[q].at[where + (slice(None), cols)], acc[q].at[(colour,) + where + (pl.ds(0, rows), slice(None))], sibling)]
+        if q == 1:
+            copies.append(remote(gvec_ref.at[where + (slice(None), cols)], acc[q].at[(colour,) + where + (pl.ds(rows, vec_rows), slice(None))], sibling))
+        return copies
+
+    swaps = [swap_copies(*piece) for piece in pieces]
+
+    def load_copies(i):
+        q, d, colour = pieces[i]
+        where = slot(colour, d)
+        cols = columns(core, colour)
+        buf = i % 3
+        copies = [pltpu.make_async_copy(sources[q].at[where + (slice(None), cols)], stage.at[buf, :, :, pl.ds(0, rows), :], load_sem.at[buf, 0])]
+        if q == 1:
+            copies.append(pltpu.make_async_copy(gvec_ref.at[where + (slice(None), cols)], stage.at[buf, :, :, pl.ds(rows, vec_rows), :], load_sem.at[buf, 1]))
+        return copies
+
+    def ring_copies(q, colour, phase):
+        order = DIM_ORDER[colour]
+        dim = order[phase]
+        rest = sorted(order[phase + 1:])
+        n_low = rows // 2
+
+        def block(d, half=None):
+            where = [None, None, None]
+            for done in order[:phase]:
+                where[done] = place[done]
+            where[dim] = lax.rem(place[dim] + d, SIDE)
+            for i, r in enumerate(rest):
+                where[r] = slice(None) if half is None or i > 0 else pl.ds(2 * half, 2)
+            tail = (slice(None), slice(None))
+            if phase == 2 and half is not None:
+                tail = (pl.ds(0, n_low) if half == 0 else pl.ds(n_low, height[q] - n_low), slice(None))
+            return acc[q].at[(colour,) + tuple(where) + tail]
+
+        def half_of(ref, direction, half):
+            if phase == 2:
+                return ref.at[colour, direction, pl.ds(0, n_low) if half == 0 else pl.ds(n_low, height[q] - n_low), :]
+            return ref.at[colour, direction, pl.ds(2 * half, 2)]
+
+        def far_of(direction, half):
+            if phase == 2:
+                return far[q][phase].at[colour, direction, pl.ds(0, n_low if half == 0 else height[q] - n_low), :]
+            return far[q][phase].at[colour, direction]
+
+        out = []
+        for direction, shift in enumerate((1, -1)):
+            device = (core, chip_at(place, dim, shift))
+            near = shift % SIDE
+            out.append(dict(
+                far=remote(block(2, direction), far_of(direction, direction), device),
+                own=remote(block(near, 1 - direction), half_of(got[q][phase], direction, 1 - direction), device),
+                fed=remote(block(near, direction), half_of(got[q][phase], direction, direction), device),
+                fed_view=block(near, direction), far_view=far_of(direction, direction)))
+        return out, block(0), [got[q][phase].at[colour, direction] for direction in range(2)]
+
+    rings = {(q, colour, phase): ring_copies(q, colour, phase) for q in range(2) for colour in range(COLOURS) for phase in range(3)}
+
+    def add_into(dst, sources, n_lead):
+        def body(i, _):
+            idx = {0: (), 1: (i,), 2: (i // SIDE, i % SIDE)}[n_lead]
+            total = dst[idx]
+            for src in sources:
+                total = total + src[idx]
+            dst[idx] = total
+            return 0
+
+        count = 1
+        for n in dst.shape[:n_lead]:
+            count *= n
+        if n_lead == 0:
+            total = dst[...]
+            for src in sources:
+                total = total + src[...]
+            dst[...] = total
+        else:
+            lax.fori_loop(0, count, body, 0)
+
+    def absorb(i):
+        q, d, colour = pieces[i]
+        for copy in load_copies(i):
+            copy.wait()
+        for copy in swaps[i]:
+            copy.wait_recv()
+        n = height[q]
+        add_into(acc[q].at[(colour,) + slot(colour, d)], [stage.at[i % 3, :, :, pl.ds(0, n), :]], 2)
+        if i + 3 < len(pieces):
+            for copy in load_copies(i + 3):
+                copy.start()
+        first = rings[(q, colour, 0)][0]
+        if d == 2:
+            start(first[0]['far'])
+            start(first[1]['far'])
+        elif d == 1:
+            start(first[0]['own'])
+        elif d == 3:
+            start(first[1]['own'])
+
+    def send_first(q, colour, phase):
+        dirs = rings[(q, colour, phase)][0]
+        for direction in dirs:
+            start(direction['far'])
+        for direction in dirs:
+            start(direction['own'])
+
+    def relay(q, colour, phase):
+        dirs = rings[(q, colour, phase)][0]
+        for direction in dirs:
+            direction['far'].wait_recv()
+            add_into(direction['fed_view'], [direction['far_view']], 2 - phase)
+        for direction in dirs:
+            start(direction['fed'])
+
+    def settle(q, colour, phase):
+        dirs, mine, arrived = rings[(q, colour, phase)]
+        for direction in dirs:
+            direction['own'].wait_recv()
+            direction['fed'].wait_recv()
+        add_into(mine, arrived, 2 - phase)
+        if phase < 2:
+            send_first(q, colour, phase + 1)
+
+    outs = (offn_ref, oattn_ref)
+    local, finals = [], []
+
+    def finish(q, colour):
+        done = acc[q].at[colour, place[0], place[1], place[2]]
+        done[...] = done[...] * scale
+        cols = columns(core, colour)
+        parts = [(done.at[pl.ds(0, rows), :], outs[q].at[:, cols])]
+        if q == 1:
+            parts.append((done.at[pl.ds(rows, vec_rows), :], ovec_ref.at[:, cols]))
+        for src, dst in parts:
+            i = counter.take()
+            keep = pltpu.make_async_copy(src, dst, load_sem.at[3 + len(local) // 2, len(local) % 2])
+            keep.start()
+            local.append(keep)
+            give = pltpu.make_async_remote_copy(src_ref=src, dst_ref=dst, send_sem=send_sem.at[i], recv_sem=recv_sem.at[i], device_id=sibling, device_id_type=MESH_ID)
+            start(give)
+            finals.append(give)
+
+    colours = range(COLOURS)
+    meet_neighbours(place)
+    for i in range(3):
+        for copy in load_copies(i):
+            copy.start()
+    for group in swaps:
+        for copy in group:
+            start(copy)
+    per_chunk = len(pieces) // 2
+    for i in range(9):
+        absorb(i)
+    for colour in colours:
+        relay(0, colour, 0)
+    for i in range(9, per_chunk + 9):
+        absorb(i)
+    for colour in colours:
+        settle(0, colour, 0)
+    for colour in colours:
+        relay(1, colour, 0)
+    for i in range(per_chunk + 9, 2 * per_chunk):
+        absorb(i)
+    for colour in colours:
+        relay(0, colour, 1)
+    for colour in colours:
+        settle(1, colour, 0)
+    for colour in colours:
+        settle(0, colour, 1)
+    for colour in colours:
+        relay(1, colour, 1)
+    for colour in colours:
+        relay(0, colour, 2)
+    for colour in colours:
+        settle(1, colour, 1)
+    for colour in colours:
+        settle(0, colour, 2)
+        finish(0, colour)
+    for colour in colours:
+        relay(1, colour, 2)
+    for colour in colours:
+        settle(1, colour, 2)
+        finish(1, colour)
+    for copy in finals:
+        copy.wait_recv()
+    for copy in started:
+        copy.wait_send()
+    for copy in local:
+        copy.wait()
+
+
+def scatter_grads(g_ffn, g_attn, g_vec, scale):
+    n_chips = SIDE ** 3
+    width = 2 * COLOURS * LANES
+    rows, vec_rows = g_ffn.shape[0] // n_chips, g_vec.shape[0] // n_chips
+    as_torus = lambda g: g.reshape(SIDE, SIDE, SIDE, g.shape[0] // n_chips, width)
+    heights = (rows, rows + vec_rows)
+    n_low = rows // 2
+    buf = lambda shape: [pltpu.VMEM((COLOURS,) + shape(h) + (LANES,), F32) for h in heights]
+    n_copies = 2 * COLOURS * 3 * 2 * 3 + 2 * COLOURS * 4 + COLOURS * 4 + 9
+    scratch = (buf(lambda h: (SIDE, SIDE, SIDE, h)) + buf(lambda h: (2, SIDE, SIDE, h)) + buf(lambda h: (2, 2, SIDE, h))
+               + buf(lambda h: (2, SIDE, h)) + buf(lambda h: (2, 2, h)) + buf(lambda h: (2, h)) + buf(lambda h: (2, max(n_low, h - n_low)))
+               + [pltpu.VMEM((3, SIDE, SIDE, heights[1], LANES), F32), pltpu.SemaphoreType.DMA((n_copies,)), pltpu.SemaphoreType.DMA((n_copies,)), pltpu.SemaphoreType.DMA((8, 2))])
+    anywhere = pl.BlockSpec(memory_space=pl.ANY)
+    sent = 4 * width * n_chips * (2 * rows + vec_rows)
+    return pl.pallas_call(
+        functools.partial(rs_kernel, scale, rows, vec_rows),
+        in_specs=[anywhere] * 3, out_specs=[anywhere] * 3,
+        out_shape=[jax.ShapeDtypeStruct((rows, width), F32), jax.ShapeDtypeStruct((rows, width), F32), jax.ShapeDtypeStruct((vec_rows, width), F32)],
+        scratch_shapes=scratch,
+        compiler_params=pltpu.CompilerParams(collective_id=1, has_side_effects=True, vmem_limit_bytes=62 * 1024 * 1024),
+        cost_estimate=pl.CostEstimate(flops=10 ** 9, bytes_accessed=2 * sent, transcendentals=0),
+        name='scatter_grads',
+    )(as_torus(g_ffn), as_torus(g_attn), as_torus(g_vec))
 
 
 def solution(mesh):
@@ -368,18 +654,14 @@
         full = lax.dynamic_update_slice_in_dim(jnp.zeros((n_own * n_fsdp,), vec_rows.dtype), mine, lax.axis_index('fsdp') * n_own, 0)
         return lax.psum(full, all_axes)
 
-    def scatter_rows(full_grad):
-        return lax.all_gather(lax.psum_scatter(full_grad, all_axes, scatter_dimension=0, tiled=True), 'dp', axis=0, tiled=True)
-
-    def scatter_vec(full_grad):
-        n_own = full_grad.shape[0] // n_fsdp
-        return lax.dynamic_slice_in_dim(lax.psum(full_grad, all_axes), lax.axis_index('fsdp') * n_own, n_own, 0)
-
     def device_step(dec_in, enc_out, src_lens, tgt_lens, y_cot, attn_w, ffn_w, vec_params):
         y_out, dec_grad, enc_grad, pairs, ffn_pairs, g_vec = layer_acts(dec_in, enc_out, src_lens, tgt_lens, y_cot, gather_rows(attn_w), gather_rows(ffn_w), gather_vec(vec_params))
         grad_scale = 1.0 / (dec_in.shape[0] * dec_in.shape[1] * n_fsdp * n_dp)
-        g_ffn = jnp.concatenate([dot_tn(lhs, rhs) for lhs, rhs in ffn_pairs], axis=0) * grad_scale
-        g_attn = jnp.concatenate([dot_tn(lhs, rhs) for lhs, rhs in pairs], axis=0) * grad_scale
-        return y_out, dec_grad, enc_grad, scatter_rows(g_attn), scatter_rows(g_ffn), scatter_vec(g_vec * grad_scale)
+        g_ffn = jnp.concatenate([dot_tn(lhs, rhs) for lhs, rhs in ffn_pairs], axis=0)
+        g_attn = jnp.concatenate([dot_tn(lhs, rhs) for lhs, rhs in pairs], axis=0)
+        n_vec = vec_params.shape[0]
+        vec_rows = jnp.pad(g_vec.reshape(n_fsdp, 1, n_vec), ((0, 0), (0, 7), (0, dec_in.shape[2] - n_vec))).reshape(n_fsdp * 8, -1)
+        ffn_out, attn_out, vec_out = scatter_grads(g_ffn, g_attn, vec_rows, grad_scale)
+        return y_out, dec_grad, enc_grad, attn_out, ffn_out, vec_out[0, :n_vec]
 
     return jax.shard_map(device_step, mesh=mesh, in_specs=(act_spec, act_spec, len_spec, len_spec, act_spec, row_spec, row_spec, vec_spec), out_specs=(act_spec, act_spec, act_spec, row_spec, row_spec, vec_spec), check_vma=False)

time: 705 us -> 423 us (0.60)
  waiting for transfers between devices: 319 us -> 17.8 us
  Pallas kernels: 166 us -> 254 us
  blocking collectives: 143 us -> 70.3 us
    reduce_scatter x2 -> x0, waiting for transfers between devices: 301 us -> none  [scatter_rows(): lax.psum_scatter(full_grad, all_axes, scatter_dimension=0, tiled=True)]
    pallas_call x0 -> x1, Pallas kernels: none -> 88 us  [scatter_grads(): pl.pallas_call(functools.partial(rs_kernel, scale, rows, vec_rows), in_sp...]
    psum x1 -> x0, blocking collectives: 64.5 us -> none  [scatter_vec(): lax.psum(full_grad, all_axes)]
    mul x3 -> x0, other arithmetic: 17.2 us -> none  [the longest x1 10.4 us: device_step(): jnp.concatenate([dot_tn(lhs, rhs) for lhs, rhs in ffn_pairs], axis=0)]
    concatenate x0 -> x1, other arithmetic: none -> 10.6 us  [device_step(): jnp.concatenate([dot_tn(lhs, rhs) for lhs, rhs in ffn_pairs], axis=0)]
    all_gather x2 -> x0, blocking collectives: 8.57 us -> none  [scatter_rows(): lax.all_gather(lax.psum_scatter(full_grad, all_axes, scatter_dimension=0,...]
  transfers between devices with their start and end apart: 4 -> 2, of which waited for: 4 -> 2; matrix products, arithmetic and copies ran while one was open for 4% -> 1% of each run, Pallas kernels for 19% -> 14%
where the time goes in v3:
time: 423 us; the launch traced here: 415 us
  Pallas kernels  254 us (60%)
  blocking collectives  70.3 us (17%)
  matrix products  33.9 us (8%)
  waiting for transfers between devices  17.8 us (4%)
  between operations  14.7 us (3%)
  local copies, waits for them, and re-layouts  13.3 us (3%)
  other arithmetic  11.4 us (3%)
    pallas_call x1, Pallas kernels, scatter_grads(): pl.pallas_call(functools.partial(rs_kernel, scale, rows, vec_rows), in_sp...  88 us
    pallas_call x2, Pallas kernels, attn_backward(): pl.pallas_call(body, grid=(n_batch, n_groups), in_specs=in_specs, out_spe...  75.6 us
    psum x1, blocking collectives, gather_vec(): return lax.psum(full, all_axes)  70.3 us
    pallas_call x2, Pallas kernels, attn_forward(): pl.pallas_call(functools.partial(attn_fwd_kernel, causal, slots), grid=(n...  57.6 us
    dot_general x10, matrix products, dot(): lax.dot_general(lhs, rhs, (contract, ((), ())), preferred_element_type=F32)  33.9 us
    pallas_call x1, Pallas kernels, ffn_both(): pl.pallas_call(ffn_kernel, grid=(n_tok // block,), in_specs=[tok, tok, on...  32.5 us
    all_gather x2, waiting for transfers between devices, gather_rows(): return lax.all_gather(mine, all_axes, axis=0, tiled=True)  17.7 us
    concatenate x1, other arithmetic, device_step(): jnp.concatenate([dot_tn(lhs, rhs) for lhs, rhs in ffn_pairs], axis=0)  10.6 us
  transfers between devices with their start and end apart: 2, of which 2 were waited for; matrix products, arithmetic and copies ran while one was open for 1% of the time, Pallas kernels for 14%

profile of v3, /device:TPU:1, one launch (start us, length us, event | category | flops | bytes accessed | tf_op | source)
XLA Modules:
  0.0 415.1 jit_solution(14044684104210910318)
XLA Ops:
  7.2 0.9 copy-done
  8.1 0.6 constant_dynamic-slice_fusion.1
  8.8 1.5 constant_dynamic-slice_fusion
  10.6 70.3 %psum.7 = bf16[14592]{0:T(1024)(128)(2,1)S(1)} all-reduce(bf16[14592]{0:T(1024)(128)(2,1)S(1)} %dynamic_update_slice.3), channel_id=1, replica_groups=mesh['dp'=2,'fsdp'=64] {'fsdp','dp'}, use_global_device_ids=true, to_apply=%region_0.1 | all-reduce | flops 14592 | bytes 58368 | tf_op jit(solution)/shard_map/psum | solution.py:655
  80.9 0.6 slice.68
  81.5 0.6 pad.8.bias_ref.rows_ref.refs_10_
  82.2 3.6 all-gather.3.cloned.1.call-done.wq_ref.wk_ref.wv_ref.wo_ref.refs_2_.refs_3_.refs_4_.refs_5_
  85.8 25.7 %attn_fwd.2 = (bf16[1024,768]{1,0:T(8,128)(2,1)}, bf16[1024,768]{1,0:T(8,128)(2,1)}, bf16[1024,768]{1,0:T(8,128)(2,1)}, bf16[1024,768]{1,0:T(8,128)(2,1)}, f32[2...) custom-call(s32[2]{0:T(128)} %refs_0_.1, ...), custom_call_target="tpu_custom_call" | custom-call | flops 11274289152 | bytes 15728640 | tf_op jit(solution)/shard_map/attn_fwd/pallas_call | solution.py:163
  111.4 32.0 %attn_fwd.3 = (bf16[1024,768]{1,0:T(8,128)(2,1)}, bf16[1536,768]{1,0:T(8,128)(2,1)}, bf16[1536,768]{1,0:T(8,128)(2,1)}, bf16[1024,768]{1,0:T(8,128)(2,1)}, f32[2...) custom-call(s32[2]{0:T(128)} %lens_ref.5, ...), custom_call_target="tpu_custom_call" | custom-call | flops 15703474176 | bytes 15728640 | tf_op jit(solution)/shard_map/attn_fwd/pallas_call | solution.py:163
  143.4 14.1 %all-gather.5.cloned.1.call-done.up_ref.down_ref = bf16[6144,768]{1,0:T(8,128)(2,1)} async-done(((bf16[48,768]{1,0:T(8,128)(2,1)}), bf16[6144,768]{1,0:T(8,128)(2,1)}) %all-gather.5.cloned.1.call-update) | async-done | bytes 9437200 | tf_op jit(solution)/shard_map/all_gather | solution.py:649
  157.5 32.5 %ffn_both.1 = (bf16[1024,768]{1,0:T(8,128)(2,1)}, bf16[1024,3072]{1,0:T(8,128)(2,1)}, bf16[1024,3072]{1,0:T(8,128)(2,1)}, bf16[1024,768]{1,0:T(8,128)(2,1)}, f32...) custom-call(bf16[1024,768]{1,0:T(8,128)(2,1)} %get-tuple-element.45.h_ref, bf16[1024,768]{1,0:T(8,128)(2,1)} %bitcast.49, ...), custom_call_target="tpu_custom_call" | custom-call | flops 19327352832 | bytes 23592960 | tf_op jit(solution)/shard_map/ffn_both/pallas_call | solution.py:316
  190.0 44.1 %attn_bwd.2 = (bf16[1024,768]{1,0:T(8,128)(2,1)}, bf16[1536,768]{1,0:T(8,128)(2,1)}, bf16[1536,768]{1,0:T(8,128)(2,1)}, f32[1024,768]{1,0:T(8,128)}, bf16[1536,7...) custom-call(s32[2]{0:T(128)} %lens_ref.5, f32[1024,768]{1,0:T(8,128)} %get-tuple-element.49.dres_ref, ...), custom_call_target="tpu_custom_call" | custom-call | flops 30198988800 | bytes 15728640 | tf_op jit(solution)/shard_map/attn_bwd/pallas_call | solution.py:264
  234.2 31.4 %attn_bwd.3 = (bf16[1024,768]{1,0:T(8,128)(2,1)}, bf16[1024,768]{1,0:T(8,128)(2,1)}, bf16[1024,768]{1,0:T(8,128)(2,1)}, bf16[1024,768]{1,0:T(8,128)(2,1)}, f32[2,8,768]{2,1,0:T(8,128)}, /*index=5*/f32[2,8,768]{2,1,0:T(8,128)}) custom-call(s32[2]{0:T(128)} %refs_0_.1, f32[1024,768]{1,0:T(8,128)} %get-tuple-element.56.refs_1_, ...), custom_call_target="tpu_custom_call" | custom-call | flops 20937965568 | bytes 15728640 | tf_op jit(solution)/shard_map/attn_bwd/pallas_call | solution.py:264
  265.6 0.8 reduce_sum.27
  267.0 1.2 pad.9
  268.2 3.0 bitcast_dynamic-update-slice_fusion.4
  271.2 7.4 %fusion.2 = f32[3072,768]{1,0:T(8,128)S(1)} fusion(bf16[1024,3072]{1,0:T(8,128)(2,1)} %get-tuple-element.63, bf16[1024,768]{1,0:T(8,128)(2,1)S(1)} %copy-done.19), kind=kOutput, calls=%fused_computation.35 | convolution fusion | flops 4831838208 | bytes 17301504 | tf_op jit(solution)/shard_map/dot_general | solution.py:20
  278.6 1.4 bitcast_dynamic-update-slice_fusion.3
  280.1 1.4 bitcast_dynamic-update-slice_fusion.2
  282.0 0.5 copy-done.12
  282.4 1.4 convolution_dynamic-update-slice_fusion.2
  284.3 1.5 convolution_dynamic-update-slice_fusion.1
  286.0 0.7 copy-done.18
  286.7 2.2 bitcast_dynamic-update-slice_fusion.1
  288.9 2.1 bitcast_dynamic-update-slice_fusion
  291.2 1.5 convolution_dynamic-update-slice_fusion
  292.7 12.0 %fusion.3 = f32[3072,768]{1,0:T(8,128)S(1)} fusion(bf16[1024,3072]{1,0:T(8,128)(2,1)} %get-tuple-element.64, bf16[1024,768]{1,0:T(8,128)(2,1)} %get-tuple-element.65), kind=kOutput, calls=%fused_computation.36 | convolution fusion | flops 4831838208 | bytes 17301504 | tf_op jit(solution)/shard_map/dot_general | solution.py:20
  304.8 10.6 %pad_maximum_fusion = f32[6144,768]{1,0:T(8,128)} fusion(f32[3072,768]{1,0:T(8,128)S(1)} %fusion.3, f32[3072,768]{1,0:T(8,128)S(1)} %fusion.2), kind=kLoop, calls=%fused_computation | loop fusion | flops 4718592 | bytes 37748736 | tf_op jit(solution)/shard_map/concatenate | solution.py:660
  315.3 88.0 %scatter_grads.1 = (f32[96,768]{1,0:T(8,128)}, f32[96,768]{1,0:T(8,128)}, f32[8,768]{1,0:T(8,128)}) custom-call(f32[4,4,4,96,768]{4,3,2,1,0:T(8,128)} %bitcast.40, f32[4,4,4,96,768]{4,3,2,1,0:T(8,128)} %bitcast.41, f32[4,4,4,8,768]{4,3,2,1,0:T(8,128)} %bitcast.42), custom_call_target="tpu_custom_call" | custom-call | flops 1000000000 | bytes 78643200 | tf_op jit(solution)/shard_map/scatter_grads/pallas_call | solution.py:625
  403.3 1.3 slice.66
  404.6 1.7 copy.36
  406.3 1.7 copy.37
  (68 shorter events, 2.1 us)
Async XLA Ops:
  7.2 0.9 copy-start
  7.2 78.6 %all-gather.3.cloned.1.call-start = ((), (), s32[]{:S(2)}) async-start(), calls=%async_computation | async-start | bytes 9510912 | tf_op jit(solution)/shard_map/all_gather | solution.py:649
  8.7 148.8 %all-gather.5.cloned.1.call-start = ((), (), s32[]{:S(2)}) async-start(), calls=%async_computation.1 | async-start | bytes 9510912 | tf_op jit(solution)/shard_map/all_gather | solution.py:649
  234.1 32.3 %copy-start.4 = (f32[2,8,768]{2,1,0:T(8,128)S(1)}, f32[2,8,768]{2,1,0:T(8,128)}, u32[]{:S(2)}) copy-start(f32[2,8,768]{2,1,0:T(8,128)} %get-tuple-element.75) | copy-start | bytes 147460
  234.1 32.4 %copy-start.3 = (f32[2,8,768]{2,1,0:T(8,128)S(1)}, f32[2,8,768]{2,1,0:T(8,128)}, u32[]{:S(2)}) copy-start(f32[2,8,768]{2,1,0:T(8,128)} %get-tuple-element.76) | copy-start | bytes 147460
  234.1 32.4 %copy-start.5 = (f32[8,768]{1,0:T(8,128)S(1)}, f32[8,768]{1,0:T(8,128)}, u32[]{:S(2)}) copy-start(f32[8,768]{1,0:T(8,128)} %get-tuple-element.77) | copy-start | bytes 73732
  234.1 32.6 %copy-start.6 = (f32[1,3072]{1,0:T(1,128)S(1)}, f32[1,3072]{1,0:T(1,128)}, u32[]{:S(2)}) copy-start(f32[1,3072]{1,0:T(1,128)} %get-tuple-element.78) | copy-start | bytes 36868
  234.1 34.1 %copy-start.8 = (bf16[2,512,768]{2,1,0:T(8,128)(2,1)S(1)}, bf16[2,512,768]{2,1,0:T(8,128)(2,1)}, u32[]{:S(2)}) copy-start(bf16[2,512,768]{2,1,0:T(8,128)(2,1)} %param.8) | copy-start | bytes 4718596
  268.2 3.0 copy-start.19
  271.2 7.4 %copy-start.16 = (bf16[1024,768]{1,0:T(8,128)(2,1)S(1)}, bf16[1024,768]{1,0:T(8,128)(2,1)}, u32[]{:S(2)}) copy-start(bf16[1024,768]{1,0:T(8,128)(2,1)} %get-tuple-element.67) | copy-start | bytes 4718596
  278.6 1.5 copy-start.15
  280.1 1.9 copy-start.10
  280.1 2.3 copy-start.12
  282.4 1.5 copy-start.11
  282.4 1.9 copy-start.14
  284.3 1.7 copy-start.7
  284.3 2.4 copy-start.18
  286.7 2.2 copy-start.17
  288.9 2.1 copy-start.9
  288.9 2.3 copy-start.13
  292.7 12.0 %copy-start.2 = (f32[6144,768]{1,0:T(8,128)}, f32[6144,768]{1,0:T(8,128)S(1)}, u32[]{:S(2)}) copy-start(f32[6144,768]{1,0:T(8,128)S(1)} %convolution_dynamic-update-slice_fusion) | copy-start | bytes 56623108
  315.3 92.7 %copy-start.1 = (bf16[96,768]{1,0:T(8,128)(2,1)S(1)}, bf16[96,768]{1,0:T(8,128)(2,1)}, u32[]{:S(2)}) copy-start(bf16[96,768]{1,0:T(8,128)(2,1)} %param.13) | copy-start | bytes 442372
Sparse Core Ops, SparseCore 0:
  11.6 74.1 all-gather.2
  89.4 68.0 all-gather.4
